TPU v7x, 32 devices: a whole 2x2x4 slice. The times are simulated.
32 devices in a mesh: part: 2 (over x), tpa: 4 (over z), tpb: 4 (over y, core).
Axes of the slice: x: 2, y: 2, z: 4, core: 2. Of those that a mesh axis runs over, the one named last changes fastest.
Arguments:
- x: bfloat16 [32, 1024, 3072], P(('part', 'tpb')), parts along dimension 0
- lengths: int32 [32], P(('part', 'tpb')), parts along dimension 0
- k_buf: bfloat16 [32, 1024, 8, 128], P(('part', 'tpb'), None, 'tpa'), parts along dimension 0
- v_buf: bfloat16 [32, 1024, 8, 128], P(('part', 'tpb'), None, 'tpa'), parts along dimension 0
- w_qkv: bfloat16 [6144, 5120], P('part', ('tpa', 'tpb')), parts along dimension 0
- w_o: bfloat16 [6144, 3072], P(('part', 'tpa', 'tpb')), parts along dimension 0
- w_gate_up: bfloat16 [6144, 16384], P('part', ('tpa', 'tpb')), parts along dimension 0
- w_down: bfloat16 [16384, 3072], P(('part', 'tpa', 'tpb')), parts along dimension 0
- g_attn: bfloat16 [6144], P('part'), parts along dimension 0
- g_mlp: bfloat16 [6144], P('part'), parts along dimension 0
Outputs:
- output 1: bfloat16 [32, 1024, 3072], P(('part', 'tpb')), parts along dimension 0
- output 2: bfloat16 [32, 1024, 8, 128], P(('part', 'tpb'), None, 'tpa'), parts along dimension 0
- output 3: bfloat16 [32, 1024, 8, 128], P(('part', 'tpb'), None, 'tpa'), parts along dimension 0
- output 4: bfloat16 [6144, 3072], P('part', 'tpa'), parts along dimension 0
- output 5: bfloat16 [6144, 1024], P('part', 'tpa'), parts along dimension 0
- output 6: bfloat16 [6144, 1024], P('part', 'tpa'), parts along dimension 0
- output 7: bfloat16 [6144, 3072], P(('part', 'tpa')), parts along dimension 0
- output 8: bfloat16 [6144, 8192], P('part', 'tpa'), parts along dimension 0
- output 9: bfloat16 [6144, 8192], P('part', 'tpa'), parts along dimension 0
- output 10: bfloat16 [16384, 3072], P(('part', 'tpa')), parts along dimension 0
There are 2 independent parts. A program takes and returns all parts, laid end to end along the dimension named above; each array names one.
All inputs are finite; a program needn't handle non-finite values.
Results may differ from a plain program's by a relative error of at most 0.0138525.
Values are sent between devices in bfloat16 or wider.
A program may use at most 1 GiB of HBM per device.

v0:
```python
import math
import jax
import jax.numpy as jnp
from jax import lax
from jax.sharding import PartitionSpec as P

ROPE_BASE = 500000.0
ROPE_FACTOR = 8.0
LOW_FREQ = 1.0
HIGH_FREQ = 4.0
ORIG_CONTEXT = 8192.0
NORM_EPS = 1e-5
MASK_VALUE = -1e30


def rms_norm(x_in, gain_vec):
    x_wide = x_in.astype(jnp.float32)
    mean_sq = jnp.mean(x_wide * x_wide, axis=-1, keepdims=True)
    return (x_wide * lax.rsqrt(mean_sq + NORM_EPS) * gain_vec.astype(jnp.float32)).astype(jnp.bfloat16)


def rope_tables(seq_len, head_dim):
    exponent = jnp.arange(head_dim // 2, dtype=jnp.float32) * (2.0 / head_dim)
    inv_freq = 1.0 / jnp.power(ROPE_BASE, exponent)
    wavelen = 2.0 * math.pi / inv_freq
    smooth = (ORIG_CONTEXT / wavelen - LOW_FREQ) / (HIGH_FREQ - LOW_FREQ)
    blended = (1.0 - smooth) * inv_freq / ROPE_FACTOR + smooth * inv_freq
    rope_freq = jnp.where(wavelen < ORIG_CONTEXT / HIGH_FREQ, inv_freq, jnp.where(wavelen > ORIG_CONTEXT / LOW_FREQ, inv_freq / ROPE_FACTOR, blended))
    angles = jnp.arange(seq_len, dtype=jnp.float32)[:, None] * rope_freq[None, :]
    return jnp.cos(angles), jnp.sin(angles)


def apply_rope(vec_in, cos_tab, sin_tab):
    half_dim = vec_in.shape[-1] // 2
    first_half = vec_in[..., :half_dim]
    second_half = vec_in[..., half_dim:]
    return jnp.concatenate([first_half * cos_tab - second_half * sin_tab, second_half * cos_tab + first_half * sin_tab], axis=-1)


def split_weights(qkv_cols, gu_cols, kv_local, head_dim, n_tpb):
    model_dim = qkv_cols.shape[0]
    group_size = qkv_cols.shape[1] // (kv_local * head_dim) - 2
    packed = qkv_cols.reshape(model_dim, kv_local, group_size + 2, head_dim)
    w_query = packed[:, :, :group_size, :].reshape(model_dim, kv_local * group_size * head_dim)
    w_key = packed[:, :, group_size, :].reshape(model_dim, kv_local * head_dim)
    w_value = packed[:, :, group_size + 1, :].reshape(model_dim, kv_local * head_dim)
    ff_block = gu_cols.shape[1] // (2 * n_tpb)
    gu_view = gu_cols.reshape(model_dim, n_tpb, 2, ff_block)
    w_gate = gu_view[:, :, 0, :].reshape(model_dim, n_tpb * ff_block)
    w_up = gu_view[:, :, 1, :].reshape(model_dim, n_tpb * ff_block)
    return w_query, w_key, w_value, w_gate, w_up


def prefill(x_loc, len_loc, k_buf, v_buf, qkv_cols, o_rows, gu_cols, down_rows, g_attn, g_mlp, n_tpb):
    batch_loc, seq_len, model_dim = x_loc.shape
    kv_local = k_buf.shape[2]
    head_dim = k_buf.shape[3]
    group_size = qkv_cols.shape[1] // (kv_local * head_dim) - 2
    x_normed = rms_norm(x_loc, g_attn)
    qkv_act = jnp.einsum('bsd,dc->bsc', x_normed, qkv_cols, preferred_element_type=jnp.float32).astype(jnp.bfloat16)
    qkv_act = qkv_act.reshape(batch_loc, seq_len, kv_local, group_size + 2, head_dim)
    cos_tab, sin_tab = rope_tables(seq_len, head_dim)
    q_rot = apply_rope(qkv_act[:, :, :, :group_size, :].astype(jnp.float32), cos_tab[:, None, None, :], sin_tab[:, None, None, :]).astype(jnp.bfloat16)
    k_rot = apply_rope(qkv_act[:, :, :, group_size, :].astype(jnp.float32), cos_tab[:, None, :], sin_tab[:, None, :]).astype(jnp.bfloat16)
    values = qkv_act[:, :, :, group_size + 1, :]
    scores = jnp.einsum('bqkgd,bskd->bkgqs', q_rot, k_rot, preferred_element_type=jnp.float32) * head_dim ** -0.5
    positions = jnp.arange(seq_len)
    allowed = (positions[None, None, :] <= positions[None, :, None]) & (positions[None, None, :] < len_loc[:, None, None])
    scores = jnp.where(allowed[:, None, None], scores, MASK_VALUE)
    attn_prob = jax.nn.softmax(scores, axis=-1).astype(jnp.bfloat16)
    attn_out = jnp.einsum('bkgqs,bskd->bqkgd', attn_prob, values, preferred_element_type=jnp.float32).astype(jnp.bfloat16)
    attn_out = attn_out.reshape(batch_loc, seq_len, kv_local * group_size * head_dim)
    attn_part = jnp.einsum('bsh,hd->bsd', attn_out, o_rows, preferred_element_type=jnp.float32).astype(jnp.bfloat16)
    attn_sum = lax.psum(attn_part, 'tpa')
    hidden = (x_loc.astype(jnp.float32) + attn_sum.astype(jnp.float32)).astype(jnp.bfloat16)
    h_normed = rms_norm(hidden, g_mlp)
    ff_block = gu_cols.shape[1] // (2 * n_tpb)
    gu_act = jnp.einsum('bsd,dc->bsc', h_normed, gu_cols, preferred_element_type=jnp.float32).astype(jnp.bfloat16)
    gu_act = gu_act.reshape(batch_loc, seq_len, n_tpb, 2, ff_block)
    mid_act = (jax.nn.silu(gu_act[..., 0, :].astype(jnp.float32)) * gu_act[..., 1, :].astype(jnp.float32)).astype(jnp.bfloat16)
    mid_act = mid_act.reshape(batch_loc, seq_len, n_tpb * ff_block)
    mlp_part = jnp.einsum('bsf,fd->bsd', mid_act, down_rows, preferred_element_type=jnp.float32).astype(jnp.bfloat16)
    mlp_sum = lax.psum(mlp_part, 'tpa')
    layer_out = (hidden.astype(jnp.float32) + mlp_sum.astype(jnp.float32)).astype(jnp.bfloat16)
    valid_pos = (positions[None, :] < len_loc[:, None])[:, :, None, None]
    k_cache = jnp.where(valid_pos, k_rot, k_buf)
    v_cache = jnp.where(valid_pos, values, v_buf)
    return layer_out, k_cache, v_cache


def solution(mesh):
    n_tpb = mesh.shape['tpb']

    def local_step(x_loc, len_loc, k_buf, v_buf, w_qkv, w_o, w_gate_up, w_down, g_attn, g_mlp):
        qkv_cols = lax.all_gather(w_qkv, 'tpb', axis=1, tiled=True)
        o_rows = lax.all_gather(w_o, 'tpb', axis=0, tiled=True)
        gu_cols = lax.all_gather(w_gate_up, 'tpb', axis=1, tiled=True)
        down_rows = lax.all_gather(w_down, 'tpb', axis=0, tiled=True)
        w_query, w_key, w_value, w_gate, w_up = split_weights(qkv_cols, gu_cols, k_buf.shape[2], k_buf.shape[3], n_tpb)
        layer_out, k_cache, v_cache = prefill(x_loc, len_loc, k_buf, v_buf, qkv_cols, o_rows, gu_cols, down_rows, g_attn, g_mlp, n_tpb)
        return (layer_out, k_cache, v_cache, w_query, w_key, w_value, o_rows, w_gate, w_up, down_rows)

    batch_spec = P(('part', 'tpb'), None, None)
    len_spec = P(('part', 'tpb'))
    cache_spec = P(('part', 'tpb'), None, 'tpa', None)
    train_cols = P('part', ('tpa', 'tpb'))
    train_rows = P(('part', 'tpa', 'tpb'), None)
    gain_spec = P('part')
    gen_cols = P('part', 'tpa')
    gen_rows = P(('part', 'tpa'), None)
    return jax.shard_map(local_step, mesh=mesh, in_specs=(batch_spec, len_spec, cache_spec, cache_spec, train_cols, train_rows, train_cols, train_rows, gain_spec, gain_spec), out_specs=(batch_spec, cache_spec, cache_spec, gen_cols, gen_cols, gen_cols, gen_rows, gen_cols, gen_cols, gen_rows), check_vma=False)
```

profile of v0, /device:TPU:0, one launch (start us, length us, event | category | flops | bytes accessed | tf_op | source)
XLA Modules:
  0.0 2684.5 jit_solution(13192888068934912249)
XLA Ops:
  7.2 0.7 all-gather.5.cloned.1.call-update
  8.0 0.7 all-gather.7.cloned.1.call-update
  9.1 10.3 fusion.2
  19.4 2.7 fusion.42
  22.8 3.6 broadcast_and_fusion
  26.4 41.4 %all-gather.5.cloned.1.call-done = bf16[3072,1280]{0,1:T(8,128)(2,1)} async-done(((bf16[3072,320]{0,1:T(8,128)(2,1)}), bf16[3072,1280]{0,1:T(8,128)(2,1)}) %all-gather.5.cloned.1.call-update) | async-done | bytes 7864336 | tf_op jit(solution)/shard_map/all_gather | solution.py:95
  67.8 40.0 %fusion.24 = bf16[4,1024,1280]{2,1,0:T(8,128)(2,1)} fusion(bf16[4,1024,3072]{2,1,0:T(8,128)(2,1)} %param.10, f32[3072]{0:T(1024)S(1)} %convert_element_type.83, f32[4,1024]{1,0:T(4,128)S(1)} %add_rsqrt_fusion.1, bf16[3072,1280]{0,1:T(8,128)(2,1)} %all-gather.5.cloned.1.call-done), kind=kOutput, calls=%fused_computation.37 | convolution fusion | flops 32267829248 | bytes 43544576 | tf_op jit(solution)/shard_map/bsd,dc->bsc/dot_general | solution.py:60
  107.8 14.3 copy.33
  122.1 4.8 fusion.53
  127.0 6.6 slice.60
  133.5 3.0 copy.58
  136.6 2.3 bitcast_convert_fusion
  138.9 8.6 copy.59
  147.5 4.3 convert_element_type.88
  151.9 3.8 subtract_convert_fusion.1
  155.7 7.3 subtract_convert_fusion
  163.0 47.3 %fusion.55 = (f32[4,2,3,1024]{3,2,1,0:T(4,128)S(1)}, f32[4,2,3,1024,1024]{3,4,2,1,0:T(8,128)}) fusion(pred[4,1024,1024]{1,2,0:T(8,128)(4,1)} %broadcast_and_fusion, bf16[4,1024,2,3,64]{4,1,3,2,0:T(8,128)(2,1)} %get-tuple-element.35, bf16[4,1024,2,3,64]{4,1,3,2,0:T(8,128)(2,1)} %get-tuple-element.34, bf16[4,1024,2,64]{3,1,2,0:T(8,128)(2,1)} %get-tuple-element.41, ...), kind=kOutput, calls=%fused_computation.75 | convolution fusion | flops 6559892480 | bytes 113344512 | tf_op jit(solution)/shard_map/sub | solution.py:70
  210.3 34.8 %fusion.32 = bf16[4,2,128,3,1024]{4,2,3,1,0:T(8,128)(2,1)} fusion(f32[4,2,3,1024,1024]{3,4,2,1,0:T(8,128)} %get-tuple-element.47, f32[4,2,3,1024]{3,2,1,0:T(4,128)S(1)} %get-tuple-element.46, bf16[4,1024,2,5,128]{1,4,3,2,0:T(8,128)(2,1)} %bitcast.67), kind=kOutput, calls=%fused_computation.49 | convolution fusion | flops 6495928320 | bytes 109150208 | tf_op jit(solution)/shard_map/bkgqs,bskd->bqkgd/dot_general | solution.py:71
  245.1 27.0 %convolution_convert_fusion.1 = bf16[4,1024,3072]{2,1,0:T(8,128)(2,1)} fusion(bf16[4,1024,768]{1,2,0:T(8,128)(2,1)} %bitcast.73, bf16[768,3072]{1,0:T(8,128)(2,1)} %all-gather.7.cloned.1.call-done), kind=kOutput, calls=%fused_computation.35 | convolution fusion | flops 19339935744 | bytes 36175872 | tf_op jit(solution)/shard_map/bsh,hd->bsd/dot_general | solution.py:73
  273.4 828.1 %all-reduce.3.cloned.1.call-done = bf16[4,1024,3072]{2,1,0:T(8,128)(2,1)} async-done(((bf16[4,1024,3072]{2,1,0:T(8,128)(2,1)}), bf16[4,1024,3072]{2,1,0:T(8,128)(2,1)}) %all-reduce.3.cloned.1.call-update) | async-done | bytes 25165840 | tf_op jit(solution)/shard_map/psum | solution.py:74
  1101.5 20.3 fusion.6
  1121.8 135.7 %all-gather.9.cloned.1.call-done = bf16[3072,4096]{1,0:T(8,128)(2,1)} async-done(((bf16[3072,1024]{1,0:T(8,128)(2,1)}), bf16[3072,4096]{1,0:T(8,128)(2,1)}) %all-gather.9.cloned.1.call-update) | async-done | bytes 25165840 | tf_op jit(solution)/shard_map/all_gather | solution.py:97
  1257.5 120.2 %convolution_convert_fusion = bf16[4,1024,4096]{2,1,0:T(8,128)(2,1)} fusion(bf16[3072,4096]{1,0:T(8,128)(2,1)} %all-gather.9.cloned.1.call-done, f32[3072]{0:T(1024)S(1)} %convert_element_type.96, f32[4,1024]{1,0:T(4,128)S(1)} %add_rsqrt_fusion, bf16[4,1024,3072]{2,1,0:T(8,128)(2,1)} %param.10, bf16[4,1024,3072]{2,1,0:T(8,128)(2,1)} %all-reduce.3.cloned.1.call-done), kind=kOutput, calls=%fused_computation.28 | convolution fusion | flops 103196655616 | bytes 109080576 | tf_op jit(solution)/shard_map/bsd,dc->bsc/dot_general | solution.py:78
  1377.7 54.4 %reshape.229 = bf16[4,1024,4,2,512]{4,3,2,1,0:T(2,128)(2,1)} reshape(bf16[4,1024,4096]{2,1,0:T(8,128)(2,1)} %convolution_convert_fusion) | data formatting | bytes 67108864 | tf_op jit(solution)/shard_map/reshape | solution.py:79
  1432.0 223.5 %fusion.15 = (f32[4,1024,4,512]{3,2,1,0:T(4,128)}, f32[4,1024,4,512]{3,2,1,0:T(4,128)}) fusion(bf16[4,1024,4,2,512]{4,3,2,1,0:T(2,128)(2,1)} %reshape.229), kind=kLoop, calls=%fused_computation.26 | loop fusion | flops 16777216 | bytes 100663296 | tf_op jit(solution)/shard_map/convert_element_type | solution.py:80
  1655.5 39.8 %reshape.234 = f32[4,1024,2048]{2,1,0:T(8,128)} reshape(f32[4,1024,4,512]{3,2,1,0:T(4,128)} %get-tuple-element.30) | data formatting | bytes 67108864 | tf_op jit(solution)/shard_map/convert_element_type | solution.py:80
  1695.3 39.8 %reshape.235 = f32[4,1024,2048]{2,1,0:T(8,128)} reshape(f32[4,1024,4,512]{3,2,1,0:T(4,128)} %get-tuple-element.31) | data formatting | bytes 67108864 | tf_op jit(solution)/shard_map/convert_element_type | solution.py:80
  1735.1 63.9 %convolution_convert_fusion.2 = bf16[4,1024,3072]{2,1,0:T(8,128)(2,1)} fusion(f32[4,1024,2048]{2,1,0:T(8,128)} %reshape.235, f32[4,1024,2048]{2,1,0:T(8,128)} %reshape.234, bf16[2048,3072]{1,0:T(8,128)(2,1)} %all-gather.11.cloned.1.call-done), kind=kOutput, calls=%fused_computation.36 | convolution fusion | flops 51602522112 | bytes 104857600 | tf_op jit(solution)/shard_map/bsf,fd->bsd/dot_general | solution.py:82
  1799.0 1.6 copy-done.1
  1800.6 2.5 copy.57
  1803.1 5.7 bitcast_select_fusion.4
  1808.9 3.5 copy.44
  1812.3 3.5 copy.45
  1815.8 5.1 slice.65
  1820.9 2.1 fusion.54
  1823.0 1.6 copy.47
  1824.6 1.6 copy.48
  1826.1 6.6 copy.46
  1832.7 41.1 %reshape.232 = bf16[3072,4,2,512]{3,2,1,0:T(2,128)(2,1)} reshape(bf16[3072,4096]{1,0:T(8,128)(2,1)} %all-gather.9.cloned.1.call-done) | data formatting | bytes 50331648 | tf_op jit(solution)/shard_map/reshape | solution.py:48
  1873.8 47.1 %fusion.52 = (bf16[3072,4,1,512]{3,2,1,0:T(2,128)(2,1)}, bf16[3072,4,1,512]{3,2,1,0:T(2,128)(2,1)}) fusion(bf16[3072,4,2,512]{3,2,1,0:T(2,128)(2,1)} %reshape.232), kind=kLoop, calls=%fused_computation.72 | loop fusion | bytes 50331648 | tf_op jit(solution)/shard_map/slice | solution.py:50
  1920.9 50.3 %copy.60 = bf16[3072,4,1,512]{0,3,1,2:T(8,128)(2,1)} copy(bf16[3072,4,1,512]{3,2,1,0:T(2,128)(2,1)} %get-tuple-element.33) | data formatting | bytes 25165824
  1971.2 16.6 copy.49
  1987.8 50.3 %copy.61 = bf16[3072,4,1,512]{0,3,1,2:T(8,128)(2,1)} copy(bf16[3072,4,1,512]{3,2,1,0:T(2,128)(2,1)} %get-tuple-element.32) | data formatting | bytes 25165824
  2038.1 16.6 copy.50
  2054.7 573.7 %all-reduce.5.cloned.1.call-done = bf16[4,1024,3072]{2,1,0:T(8,128)(2,1)} async-done(((bf16[4,1024,3072]{2,1,0:T(8,128)(2,1)}), bf16[4,1024,3072]{2,1,0:T(8,128)(2,1)}) %all-reduce.5.cloned.1.call-update) | async-done | bytes 25165840 | tf_op jit(solution)/shard_map/psum | solution.py:83
  2628.4 33.4 %fusion.9 = bf16[4,1024,3072]{2,1,0:T(8,128)(2,1)} fusion(bf16[4,1024,3072]{2,1,0:T(8,128)(2,1)} %all-reduce.5.cloned.1.call-done, bf16[4,1024,3072]{2,1,0:T(8,128)(2,1)} %all-reduce.3.cloned.1.call-done, bf16[4,1024,3072]{2,1,0:T(8,128)(2,1)} %param.10), kind=kLoop, calls=%fused_computation.18 | loop fusion | flops 100663296 | bytes 100663296 | tf_op jit(solution)/shard_map/convert_element_type | solution.py:84
  2661.8 4.8 copy.68
  2666.7 10.5 copy.69
  (36 shorter events, 2.4 us)
Async XLA Ops:
  7.2 60.7 %all-gather.5.cloned.1.call-start = ((), (), s32[]{:S(2)}) async-start(), calls=%async_computation | async-start | bytes 9830400 | tf_op jit(solution)/shard_map/all_gather | solution.py:95
  7.9 237.2 %all-gather.7.cloned.1.call-start = ((), (), s32[]{:S(2)}) async-start(), calls=%async_computation.1 | async-start | bytes 5898240 | tf_op jit(solution)/shard_map/all_gather | solution.py:96
  8.7 1092.8 %all-reduce.3.cloned.1.call-start = ((), (), s32[]{:S(2)}) async-start(), calls=%async_computation.2 | async-start | bytes 50331648 | tf_op jit(solution)/shard_map/psum | solution.py:74
  9.0 10.4 copy-start.6
  9.1 13.1 copy-start.8
  22.2 0.6 copy-start.4
  147.5 4.4 copy-start
  151.8 3.8 copy-start.3
  155.7 7.3 copy-start.2
  272.1 1.2 copy-start.7
  272.1 985.3 %all-gather.9.cloned.1.call-start = ((), (), s32[]{:S(2)}) async-start(), calls=%async_computation.3 | async-start | bytes 31457280 | tf_op jit(solution)/shard_map/all_gather | solution.py:97
  272.7 1462.4 %all-gather.11.cloned.1.call-start = ((), (), s32[]{:S(2)}) async-start(), calls=%async_computation.4 | async-start | bytes 15728640 | tf_op jit(solution)/shard_map/all_gather | solution.py:98
  273.3 2355.1 %all-reduce.5.cloned.1.call-start = ((), (), s32[]{:S(2)}) async-start(), calls=%async_computation.5 | async-start | bytes 50331648 | tf_op jit(solution)/shard_map/psum | solution.py:83
  1799.0 1.6 copy-start.1
  1799.0 4.1 copy-start.5
Sparse Core Ops, SparseCore 0:
  9.5 58.2 all-gather.4
  69.4 37.2 all-gather.6
  272.3 829.1 all-reduce.2
  1102.9 154.5 all-gather.8
  1258.9 82.7 all-gather.10
  1799.1 829.1 all-reduce.4
where the time goes:
time: 2700 us; the launch traced here: 2680 us
  waiting for transfers between devices  1580 us (59%)
  local copies, waits for them, and re-layouts  437 us (16%)
  matrix products  333 us (12%)
  other arithmetic  318 us (12%)
    psum x1, waiting for transfers between devices, prefill(): attn_sum = lax.psum(attn_part, 'tpa')  828 us
    psum x1, waiting for transfers between devices, prefill(): mlp_sum = lax.psum(mlp_part, 'tpa')  574 us
    convert_element_type x1, other arithmetic, prefill(): gu_act[..., 0, :].astype(jnp.float32)  224 us
    unnamed x32, local copies, waits for them, and re-layouts  182 us
    all_gather x1, waiting for transfers between devices, local_step(): gu_cols = lax.all_gather(w_gate_up, 'tpb', axis=1, tiled=True)  136 us
    dot_general x1, matrix products, prefill(): jnp.einsum('bsd,dc->bsc', h_normed, gu_cols, preferred_element_type=jnp.f...  120 us
    dot_general x1, matrix products, prefill(): jnp.einsum('bsf,fd->bsd', mid_act, down_rows, preferred_element_type=jnp....  63.9 us
    reshape x1, local copies, waits for them, and re-layouts, prefill(): gu_act = gu_act.reshape(batch_loc, seq_len, n_tpb, 2, ff_block)  54.4 us
  transfers between devices with their start and end apart: 6, of which 4 were waited for; matrix products, arithmetic and copies ran while one was open for 35% of the time, Pallas kernels for 0%

commit v1 on v0

v1 whole, which is shorter than its diff:
```python
import math
import jax
import jax.numpy as jnp
from jax import lax
from jax.experimental import pallas as pl
from jax.sharding import PartitionSpec as P

ROPE_BASE = 500000.0
ROPE_FACTOR = 8.0
LOW_FREQ = 1.0
HIGH_FREQ = 4.0
ORIG_CONTEXT = 8192.0
NORM_EPS = 1e-5
MASK_VALUE = -1e30


def rms_norm(x_in, gain_vec):
    x_wide = x_in.astype(jnp.float32)
    mean_sq = jnp.mean(x_wide * x_wide, axis=-1, keepdims=True)
    return (x_wide * lax.rsqrt(mean_sq + NORM_EPS) * gain_vec.astype(jnp.float32)).astype(jnp.bfloat16)


def rope_tables(seq_len, head_dim):
    exponent = jnp.arange(head_dim // 2, dtype=jnp.float32) * (2.0 / head_dim)
    inv_freq = 1.0 / jnp.power(ROPE_BASE, exponent)
    wavelen = 2.0 * math.pi / inv_freq
    smooth = (ORIG_CONTEXT / wavelen - LOW_FREQ) / (HIGH_FREQ - LOW_FREQ)
    blended = (1.0 - smooth) * inv_freq / ROPE_FACTOR + smooth * inv_freq
    rope_freq = jnp.where(wavelen < ORIG_CONTEXT / HIGH_FREQ, inv_freq, jnp.where(wavelen > ORIG_CONTEXT / LOW_FREQ, inv_freq / ROPE_FACTOR, blended))
    angles = jnp.arange(seq_len, dtype=jnp.float32)[:, None] * rope_freq[None, :]
    return jnp.cos(angles), jnp.sin(angles)


def apply_rope(vec_in, cos_tab, sin_tab):
    half_dim = vec_in.shape[-1] // 2
    first_half = vec_in[..., :half_dim]
    second_half = vec_in[..., half_dim:]
    return jnp.concatenate([first_half * cos_tab - second_half * sin_tab, second_half * cos_tab + first_half * sin_tab], axis=-1)


ROW_SPLIT = 2


def split_qkv(qkv_cols, kv_local, head_dim):
    model_dim = qkv_cols.shape[0]
    group_size = qkv_cols.shape[1] // (kv_local * head_dim) - 2
    packed = qkv_cols.reshape(model_dim, kv_local, group_size + 2, head_dim)
    w_query = packed[:, :, :group_size, :].reshape(model_dim, kv_local * group_size * head_dim)
    w_key = packed[:, :, group_size, :].reshape(model_dim, kv_local * head_dim)
    w_value = packed[:, :, group_size + 1, :].reshape(model_dim, kv_local * head_dim)
    return w_query, w_key, w_value


def dot_f32(lhs, rhs):
    return jnp.dot(lhs, rhs, preferred_element_type=jnp.float32)


def add_bf16(a, b):
    return lax.reduce_precision(a.astype(jnp.float32) + b.astype(jnp.float32), 8, 7).astype(jnp.bfloat16)


def inward(part, axis):
    return lax.ppermute(part, axis, [(0, 1), (3, 2)])


def across(part, axis):
    return lax.ppermute(part, axis, [(1, 2), (2, 1)])


def outward(total, axis):
    got = lax.ppermute(total, axis, [(1, 0), (2, 3)])
    place = lax.axis_index(axis)
    return jnp.where((place == 0) | (place == 3), got, total)


tie = lax.optimization_barrier


def settle(array):
    rows, cols = array.shape
    block = pl.BlockSpec((min(rows, 256), cols), lambda i: (i, 0))

    def body(src_ref, dst_ref):
        dst_ref[...] = src_ref[...]

    return pl.pallas_call(body, grid=(rows // min(rows, 256),), in_specs=[block], out_specs=block, out_shape=jax.ShapeDtypeStruct(array.shape, array.dtype), cost_estimate=pl.CostEstimate(flops=10**9, bytes_accessed=4 * rows * cols, transcendentals=0))(array)


def line_items(n_chunks, rows):
    items = [('attn', c, 0, rows) for c in range(n_chunks)]
    for c in range(n_chunks):
        pieces = {n_chunks - 1: 4, n_chunks - 2: 2}.get(c, 1)
        items += [('mlp', c, i, rows // pieces) for i in range(0, rows, rows // pieces)]
    return items


def attention(x_prompt, length, qkv_cols, o_rows, g_attn, cos_tab, sin_tab, kv_local, head_dim):
    seq_len = x_prompt.shape[0]
    group_size = qkv_cols.shape[1] // (kv_local * head_dim) - 2
    qkv_act = dot_f32(rms_norm(x_prompt, g_attn), qkv_cols).astype(jnp.bfloat16)
    qkv_act = qkv_act.reshape(seq_len, kv_local, group_size + 2, head_dim)
    q_rot = apply_rope(qkv_act[:, :, :group_size, :].astype(jnp.float32), cos_tab[:, None, None, :], sin_tab[:, None, None, :]).astype(jnp.bfloat16)
    k_rot = apply_rope(qkv_act[:, :, group_size, :].astype(jnp.float32), cos_tab[:, None, :], sin_tab[:, None, :]).astype(jnp.bfloat16)
    values = qkv_act[:, :, group_size + 1, :]
    scores = jnp.einsum('qkgd,skd->kgqs', q_rot, k_rot, preferred_element_type=jnp.float32) * head_dim ** -0.5
    positions = jnp.arange(seq_len)
    allowed = (positions[None, :] <= positions[:, None]) & (positions[None, :] < length)
    scores = jnp.where(allowed[None, None], scores, MASK_VALUE)
    attn_prob = jax.nn.softmax(scores, axis=-1).astype(jnp.bfloat16)
    attn_out = jnp.einsum('kgqs,skd->qkgd', attn_prob, values, preferred_element_type=jnp.float32).astype(jnp.bfloat16)
    attn_out = attn_out.reshape(seq_len, kv_local * group_size * head_dim)
    return dot_f32(attn_out, o_rows).astype(jnp.bfloat16), k_rot, values


def mlp(hidden, w_gate, w_up, down_rows, g_mlp):
    h_normed = rms_norm(hidden, g_mlp)
    gate_act = dot_f32(h_normed, w_gate).astype(jnp.bfloat16)
    up_act = dot_f32(h_normed, w_up).astype(jnp.bfloat16)
    mid_act = (jax.nn.silu(gate_act.astype(jnp.float32)) * up_act.astype(jnp.float32)).astype(jnp.bfloat16)
    return dot_f32(mid_act, down_rows).astype(jnp.bfloat16)


def residual(base, delta):
    return (base.astype(jnp.float32) + delta.astype(jnp.float32)).astype(jnp.bfloat16)


def solution(mesh):
    assert mesh.shape['tpa'] == 4

    def one_layer(x_loc, len_loc, k_buf, v_buf, w_qkv, w_o, w_gate_up, w_down, g_attn, g_mlp):
        batch_loc, seq_len, _ = x_loc.shape
        kv_local, head_dim = k_buf.shape[2], k_buf.shape[3]
        ff_block = w_gate_up.shape[1] // 2
        qkv_cols = lax.all_gather(w_qkv, 'tpb', axis=1, tiled=True)
        w_o, qkv_cols = lax.optimization_barrier((w_o, qkv_cols))
        o_rows = lax.all_gather(w_o, 'tpb', axis=0, tiled=True)
        w_gate_up, o_rows = lax.optimization_barrier((w_gate_up, o_rows))
        w_gate = lax.all_gather(w_gate_up[:, :ff_block], 'tpb', axis=1, tiled=True)
        w_up = lax.all_gather(w_gate_up[:, ff_block:], 'tpb', axis=1, tiled=True)
        w_down, w_up = lax.optimization_barrier((w_down, w_up))
        down_rows = lax.all_gather(w_down, 'tpb', axis=0, tiled=True)
        cos_tab, sin_tab = rope_tables(seq_len, head_dim)
        layer_out = jnp.zeros_like(x_loc)
        rows = seq_len // ROW_SPLIT
        k_new, v_new = [], []
        chunks = [(b, r) for b in range(batch_loc) for r in range(0, seq_len, rows)]
        n_chunks = len(chunks)
        items = line_items(n_chunks, rows)
        n_items = len(items)
        first, total, mlp_part, hidden = {}, {}, {}, {}
        waiting, settled = {'o': o_rows, 'gate': w_gate, 'up': w_up, 'down': down_rows}, {}
        x_prompt = {b: x_loc[b] for b in range(batch_loc)}
        attn_part = None
        for t in range(n_items + 2):
            if t < n_items:
                kind, c, start, size = items[t]
                if kind == 'attn':
                    b, r = chunks[c]
                    if r == 0:
                        attn_part, k_rot, values = attention(x_prompt[b], len_loc[b], qkv_cols, o_rows, g_attn, cos_tab, sin_tab, kv_local, head_dim)
                        if b + 1 < batch_loc:
                            x_prompt[b + 1], attn_part, k_rot, values = tie((x_prompt[b + 1], attn_part, k_rot, values))
                        k_new.append(k_rot)
                        v_new.append(values)
                    part = attn_part[r:r + rows]
                else:
                    part = mlp_part[c][start:start + size]
                got = inward(part, 'tpa')
            if t >= 1 and t - 1 < n_items:
                if t < n_items:
                    if t + 1 < batch_loc:
                        part, first[t - 1], x_prompt[t + 1] = tie((part, first[t - 1], x_prompt[t + 1]))
                    else:
                        part, first[t - 1] = tie((part, first[t - 1]))
                crossed = across(first[t - 1], 'tpa')
                total_next = add_bf16(first[t - 1], crossed)
            if t >= 2:
                if t < n_items:
                    part, total[t - 2] = tie((part, total[t - 2]))
                kind, c, start, size = items[t - 2]
                b, r = chunks[c]
                summed = outward(total[t - 2], 'tpa')
                if kind == 'attn':
                    x_rows, summed = tie((x_loc[b, r:r + rows], summed))
                    hidden[c] = residual(x_rows, summed)
                    mlp_part[c] = mlp(hidden[c], w_gate, w_up, down_rows, g_mlp)
                else:
                    piece = residual(hidden[c][start:start + size], summed)
                    layer_out = lax.dynamic_update_slice(layer_out, piece[None], (b, r + start, 0))
            if 3 <= t < n_items and items[t - 3][0] == 'attn':
                c = items[t - 3][1]
                part, mlp_part[c] = tie((part, mlp_part[c]))
                name = {2: 'o', 3: 'gate', 4: 'up', 5: 'down'}.get(c)
                if name:
                    waiting[name], mlp_part[c] = tie((waiting[name], mlp_part[c]))
                    settled[name] = settle(waiting[name])
                    part, settled[name] = tie((part, settled[name]))
                if c == n_chunks - 3:
                    qkv_cols, mlp_part[c] = tie((qkv_cols, mlp_part[c]))
            if t < n_items:
                first[t] = add_bf16(part, got)
            if t >= 1 and t - 1 < n_items:
                total[t - 1] = total_next
        valid_pos = (jnp.arange(seq_len)[None, :] < len_loc[:, None])[:, :, None, None]
        k_cache = jnp.where(valid_pos, jnp.stack(k_new), k_buf)
        v_cache = jnp.where(valid_pos, jnp.stack(v_new), v_buf)
        w_query, w_key, w_value = split_qkv(qkv_cols, kv_local, head_dim)
        return (layer_out, k_cache, v_cache, w_query, w_key, w_value, settled['o'], settled['gate'], settled['up'], settled['down'])

    batch_spec = P(('part', 'tpb'), None, None)
    len_spec = P(('part', 'tpb'))
    cache_spec = P(('part', 'tpb'), None, 'tpa', None)
    train_cols = P('part', ('tpa', 'tpb'))
    train_rows = P(('part', 'tpa', 'tpb'), None)
    gain_spec = P('part')
    gen_cols = P('part', 'tpa')
    gen_rows = P(('part', 'tpa'), None)
    return jax.shard_map(one_layer, mesh=mesh, in_specs=(batch_spec, len_spec, cache_spec, cache_spec, train_cols, train_rows, train_cols, train_rows, gain_spec, gain_spec), out_specs=(batch_spec, cache_spec, cache_spec, gen_cols, gen_cols, gen_cols, gen_rows, gen_cols, gen_cols, gen_rows), check_vma=False)
```

time: 2700 us -> 2090 us (0.77)
  waiting for transfers between devices: 1580 us -> 711 us
  starting transfers between devices: 0.23 us -> 408 us
  local copies, waits for them, and re-layouts: 437 us -> 165 us
  matrix products: 333 us -> 434 us
  Pallas kernels: 0 us -> 43.1 us
    psum x2 -> x0, waiting for transfers between devices: 1400 us -> none  [the longest x1 828 us: prefill(): attn_sum = lax.psum(attn_part, 'tpa')]
    ppermute x0 -> x60, waiting for transfers between devices: none -> 620 us  [the longest x20 573 us: outward(): got = lax.ppermute(total, axis, [(1, 0), (2, 3)])]
    ppermute x0 -> x60, starting transfers between devices: none -> 407 us  [the longest x20 341 us: inward(): return lax.ppermute(part, axis, [(0, 1), (3, 2)])]
    unnamed x32 -> x235, local copies, waits for them, and re-layouts: 182 us -> 57.9 us
    reshape x2 -> x0, local copies, waits for them, and re-layouts: 95.4 us -> none  [the longest x1 54.4 us: prefill(): gu_act = gu_act.reshape(batch_loc, seq_len, n_tpb, 2, ff_block)]
    all_gather x4 -> x5, waiting for transfers between devices: 177 us -> 90.6 us  [the longest x1 59.6 us: one_layer(): qkv_cols = lax.all_gather(w_qkv, 'tpb', axis=1, tiled=True)]
    dot_general x5 -> x36, matrix products: 286 us -> 365 us  [the longest x32 323 us: dot_f32(): return jnp.dot(lhs, rhs, preferred_element_type=jnp.float32)]
    convert_element_type x3 -> x4, local copies, waits for them, and re-layouts: 93.9 us -> 17.8 us  [attention(): qkv_act = dot_f32(rms_norm(x_prompt, g_attn), qkv_cols).astype(jnp.bfloat16)]
  transfers between devices with their start and end apart: 6 -> 65, of which waited for: 4 -> 22; matrix products, arithmetic and copies ran while one was open for 35% -> 41% of each run, Pallas kernels for 0% -> 2%
where the time goes in v1:
time: 2090 us; the launch traced here: 2070 us
  waiting for transfers between devices  711 us (34%)
  matrix products  434 us (21%)
  starting transfers between devices  408 us (20%)
  other arithmetic  296 us (14%)
  local copies, waits for them, and re-layouts  165 us (8%)
  Pallas kernels  43.1 us (2%)
    ppermute x20, waiting for transfers between devices, outward(): got = lax.ppermute(total, axis, [(1, 0), (2, 3)])  573 us
    ppermute x20, starting transfers between devices, inward(): return lax.ppermute(part, axis, [(0, 1), (3, 2)])  341 us
    dot_general x32, matrix products, dot_f32(): return jnp.dot(lhs, rhs, preferred_element_type=jnp.float32)  323 us
    convert_element_type x40, other arithmetic, add_bf16(): lax.reduce_precision(a.astype(jnp.float32) + b.astype(jnp.float32), 8, 7)  176 us
    sub x4, matrix products, attention(): attn_prob = jax.nn.softmax(scores, axis=-1).astype(jnp.bfloat16)  68.3 us
    all_gather x1, waiting for transfers between devices, one_layer(): qkv_cols = lax.all_gather(w_qkv, 'tpb', axis=1, tiled=True)  59.6 us
    unnamed x235, local copies, waits for them, and re-layouts  57.9 us
    ppermute x20, waiting for transfers between devices, inward(): return lax.ppermute(part, axis, [(0, 1), (3, 2)])  46.9 us
  transfers between devices with their start and end apart: 65, of which 22 were waited for; matrix products, arithmetic and copies ran while one was open for 41% of the time, Pallas kernels for 2%

profile of v1, /device:TPU:0, one launch (start us, length us, event | category | flops | bytes accessed | tf_op | source)
XLA Modules:
  0.0 2072.9 jit_solution(4063116581625228327)
XLA Ops:
  8.0 59.6 %all-gather.6.cloned.1.call-done = bf16[3072,1280]{0,1:T(8,128)(2,1)} async-done(((bf16[3072,320]{0,1:T(8,128)(2,1)}), bf16[3072,1280]{0,1:T(8,128)(2,1)}) %all-gather.6.cloned.1.call-update) | async-done | bytes 7864336 | tf_op jit(solution)/shard_map/all_gather | solution.py:134
  75.6 31.0 %all-gather.8.cloned.1.call-done.src_ref = bf16[768,3072]{1,0:T(8,128)(2,1)} async-done(((bf16[192,3072]{1,0:T(8,128)(2,1)}), bf16[768,3072]{1,0:T(8,128)(2,1)}) %all-gather.8.cloned.1.call-update) | async-done | bytes 4718608 | tf_op jit(solution)/shard_map/all_gather | solution.py:136
  119.9 15.9 slice_bitcast_fusion
  135.9 17.9 slice_bitcast_fusion.3
  153.8 11.8 fusion.137
  185.4 16.1 fusion.260
  265.3 18.2 fusion.265
  283.5 10.3 fusion.161
  319.1 46.8 %collective-permute-done.1 = bf16[512,3072]{1,0:T(8,128)(2,1)} collective-permute-done((bf16[512,3072]{1,0:T(8,128)(2,1)}, bf16[512,3072]{1,0:T(8,128)(2,1)}, u32[]{:S(2)}, u32[]{:S(2)}) %collective-permute-start.1) | collective-permute-done | bytes 3145760 | tf_op jit(solution)/shard_map/ppermute | solution.py:63
  404.1 16.2 fusion.270
  485.2 17.8 fusion.275
  503.0 11.5 fusion.159
  544.9 46.4 %collective-permute-done.3 = bf16[512,3072]{1,0:T(8,128)(2,1)S(1)} collective-permute-done((bf16[512,3072]{1,0:T(8,128)(2,1)S(1)}, bf16[512,3072]{1,0:T(8,128)(2,1)S(1)}, u32[]{:S(2)}, u32[]{:S(2)}) %collective-permute-start.3) | collective-permute-done | bytes 3145760 | tf_op jit(solution)/shard_map/ppermute | solution.py:71
  594.0 62.6 %collective-permute-done.8 = bf16[512,3072]{1,0:T(8,128)(2,1)S(1)} collective-permute-done((bf16[512,3072]{1,0:T(8,128)(2,1)S(1)}, bf16[512,3072]{1,0:T(8,128)(2,1)S(1)}, u32[]{:S(2)}, u32[]{:S(2)}) %collective-permute-start.8) | collective-permute-done | bytes 3145760 | tf_op jit(solution)/shard_map/ppermute | solution.py:71
  678.4 12.5 fusion.127
  691.0 10.7 convolution_convert_fusion.24
  701.7 12.9 convolution_convert_fusion.11
  719.8 12.1 fusion.126
  759.9 41.6 %collective-permute-done.11 = bf16[512,3072]{1,0:T(8,128)(2,1)S(1)} collective-permute-done((bf16[512,3072]{1,0:T(8,128)(2,1)S(1)}, bf16[512,3072]{1,0:T(8,128)(2,1)S(1)}, u32[]{:S(2)}, u32[]{:S(2)}) %collective-permute-start.11) | collective-permute-done | bytes 3145760 | tf_op jit(solution)/shard_map/ppermute | solution.py:71
  826.4 10.8 convolution_convert_fusion.9
  880.9 10.3 convolution_convert_fusion.20
  900.9 10.8 convolution_convert_fusion.8
  911.8 13.2 shard_map.178
  968.9 10.8 convolution_convert_fusion.7
  979.8 13.2 shard_map.179
  1003.8 11.4 collective-permute-done.20
  1020.7 10.6 convolution_convert_fusion.16
  1045.0 12.0 convolution_convert_fusion.6
  1057.0 11.4 shard_map.180
  1098.8 70.3 %collective-permute-start.24 = (bf16[512,3072]{1,0:T(8,128)(2,1)}, bf16[512,3072]{1,0:T(8,128)(2,1)}, u32[]{:S(2)}, u32[]{:S(2)}) collective-permute-start(bf16[512,3072]{1,0:T(8,128)(2,1)} %convolution_convert_fusion.10), channel_id=1, source_target_pairs={{0,4},{12,8},{1,5},{13,9},{2,6},{14,10},{3,7},{15,11},{16,20},{28,... | collective-permute-start | bytes 9437192 | tf_op jit(solution)/shard_map/ppermute | solution.py:63
  1184.1 29.7 %collective-permute-done.27 = bf16[512,3072]{1,0:T(8,128)(2,1)} collective-permute-done((bf16[512,3072]{1,0:T(8,128)(2,1)}, bf16[512,3072]{1,0:T(8,128)(2,1)}, u32[]{:S(2)}, u32[]{:S(2)}) %collective-permute-start.27) | collective-permute-done | bytes 3145760 | tf_op jit(solution)/shard_map/ppermute | solution.py:71
  1216.9 57.6 %collective-permute-done.23 = bf16[512,3072]{1,0:T(8,128)(2,1)} collective-permute-done((bf16[512,3072]{1,0:T(8,128)(2,1)S(1)}, bf16[512,3072]{1,0:T(8,128)(2,1)}, u32[]{:S(2)}, u32[]{:S(2)}) %collective-permute-start.23) | collective-permute-done | bytes 3145760 | tf_op jit(solution)/shard_map/ppermute | solution.py:71
  1287.2 12.2 convolution_convert_fusion.14
  1326.4 13.5 convolution_convert_fusion.5
  1391.1 47.4 %collective-permute-start.40 = (bf16[256,3072]{1,0:T(8,128)(2,1)}, bf16[256,3072]{1,0:T(8,128)(2,1)}, u32[]{:S(2)}, u32[]{:S(2)}) collective-permute-start(bf16[256,3072]{1,0:T(8,128)(2,1)} %get-tuple-element.264), channel_id=1, source_target_pairs={{0,4},{12,8},{1,5},{13,9},{2,6},{14,10},{3,7},{15,11},{16,20},{28,... | collective-permute-start | bytes 4718600 | tf_op jit(solution)/shard_map/ppermute | solution.py:63
  1461.5 20.4 collective-permute-done.26
  1481.9 30.0 %collective-permute-start.43 = (bf16[256,3072]{1,0:T(8,128)(2,1)}, bf16[256,3072]{1,0:T(8,128)(2,1)}, u32[]{:S(2)}, u32[]{:S(2)}) collective-permute-start(bf16[256,3072]{1,0:T(8,128)(2,1)} %get-tuple-element.269), channel_id=1, source_target_pairs={{0,4},{12,8},{1,5},{13,9},{2,6},{14,10},{3,7},{15,11},{16,20},{28,... | collective-permute-start | bytes 4718600 | tf_op jit(solution)/shard_map/ppermute | solution.py:63
  1535.1 90.0 %collective-permute-start.46 = (bf16[128,3072]{1,0:T(8,128)(2,1)}, bf16[128,3072]{1,0:T(8,128)(2,1)}, u32[]{:S(2)}, u32[]{:S(2)}) collective-permute-start(bf16[128,3072]{1,0:T(8,128)(2,1)} %get-tuple-element.273), channel_id=1, source_target_pairs={{0,4},{12,8},{1,5},{13,9},{2,6},{14,10},{3,7},{15,11},{16,20},{28,... | collective-permute-start | bytes 2359304 | tf_op jit(solution)/shard_map/ppermute | solution.py:63
  1645.1 38.4 %collective-permute-done.33 = bf16[512,3072]{1,0:T(8,128)(2,1)} collective-permute-done((bf16[512,3072]{1,0:T(8,128)(2,1)}, bf16[512,3072]{1,0:T(8,128)(2,1)}, u32[]{:S(2)}, u32[]{:S(2)}) %collective-permute-start.33) | collective-permute-done | bytes 3145760 | tf_op jit(solution)/shard_map/ppermute | solution.py:71
  1695.3 39.3 %collective-permute-start.52 = (bf16[128,3072]{1,0:T(8,128)(2,1)}, bf16[128,3072]{1,0:T(8,128)(2,1)}, u32[]{:S(2)}, u32[]{:S(2)}) collective-permute-start(bf16[128,3072]{1,0:T(8,128)(2,1)} %get-tuple-element.281), channel_id=1, source_target_pairs={{0,4},{12,8},{1,5},{13,9},{2,6},{14,10},{3,7},{15,11},{16,20},{28,... | collective-permute-start | bytes 2359304 | tf_op jit(solution)/shard_map/ppermute | solution.py:63
  1750.3 40.3 %collective-permute-done.36 = bf16[512,3072]{1,0:T(8,128)(2,1)S(1)} collective-permute-done((bf16[512,3072]{1,0:T(8,128)(2,1)}, bf16[512,3072]{1,0:T(8,128)(2,1)S(1)}, u32[]{:S(2)}, u32[]{:S(2)}) %collective-permute-start.36) | collective-permute-done | bytes 3145760 | tf_op jit(solution)/shard_map/ppermute | solution.py:71
  1817.8 47.7 %collective-permute-done.39 = bf16[512,3072]{1,0:T(8,128)(2,1)} collective-permute-done((bf16[512,3072]{1,0:T(8,128)(2,1)}, bf16[512,3072]{1,0:T(8,128)(2,1)}, u32[]{:S(2)}, u32[]{:S(2)}) %collective-permute-start.39) | collective-permute-done | bytes 3145760 | tf_op jit(solution)/shard_map/ppermute | solution.py:71
  1878.9 54.0 %collective-permute-done.42 = bf16[512,3072]{1,0:T(8,128)(2,1)} collective-permute-done((bf16[512,3072]{1,0:T(8,128)(2,1)}, bf16[512,3072]{1,0:T(8,128)(2,1)}, u32[]{:S(2)}, u32[]{:S(2)}) %collective-permute-start.42) | collective-permute-done | bytes 3145760 | tf_op jit(solution)/shard_map/ppermute | solution.py:71
  1938.8 27.8 %collective-permute-done.45 = bf16[256,3072]{1,0:T(8,128)(2,1)} collective-permute-done((bf16[256,3072]{1,0:T(8,128)(2,1)}, bf16[256,3072]{1,0:T(8,128)(2,1)}, u32[]{:S(2)}, u32[]{:S(2)}) %collective-permute-start.45) | collective-permute-done | bytes 1572896 | tf_op jit(solution)/shard_map/ppermute | solution.py:71
  1970.6 29.7 %collective-permute-done.48 = bf16[256,3072]{1,0:T(8,128)(2,1)} collective-permute-done((bf16[256,3072]{1,0:T(8,128)(2,1)}, bf16[256,3072]{1,0:T(8,128)(2,1)}, u32[]{:S(2)}, u32[]{:S(2)}) %collective-permute-start.48) | collective-permute-done | bytes 1572896 | tf_op jit(solution)/shard_map/ppermute | solution.py:71
  2002.5 14.6 collective-permute-done.51
  2018.6 15.3 collective-permute-done.54
  2035.5 12.8 collective-permute-done.56
  (529 shorter events, 779.0 us)
Async XLA Ops:
  7.9 98.7 %all-gather.8.cloned.1.call-start = ((), (), s32[]{:S(2)}) async-start(), calls=%async_computation.1 | async-start | bytes 5898240 | tf_op jit(solution)/shard_map/all_gather | solution.py:136
  67.7 416.3 %all-gather.12.cloned.1.call-start = ((), (), s32[]{:S(2)}) async-start(), calls=%async_computation.3 | async-start | bytes 15728640 | tf_op jit(solution)/shard_map/all_gather | solution.py:139
  112.6 565.9 %all-gather.10.cloned.1.call-start = ((), (), s32[]{:S(2)}) async-start(), calls=%async_computation.2 | async-start | bytes 15728640 | tf_op jit(solution)/shard_map/all_gather | solution.py:138
  225.8 77.5 %collective-permute-start = (bf16[512,3072]{1,0:T(8,128)(2,1)}, bf16[512,3072]{1,0:T(8,128)(2,1)}, u32[]{:S(2)}, u32[]{:S(2)}) collective-permute-start(bf16[512,3072]{1,0:T(8,128)(2,1)} %get-tuple-element.355), channel_id=1, source_target_pairs={{0,4},{12,8},{1,5},{13,9},{2,6},{14,10},{3,7},{15,11},{16,20},{28,... | collective-permute-start | bytes 9437192 | tf_op jit(solution)/shard_map/ppermute | solution.py:63
  258.0 107.9 %collective-permute-start.1 = (bf16[512,3072]{1,0:T(8,128)(2,1)}, bf16[512,3072]{1,0:T(8,128)(2,1)}, u32[]{:S(2)}, u32[]{:S(2)}) collective-permute-start(bf16[512,3072]{1,0:T(8,128)(2,1)} %get-tuple-element.161), channel_id=1, source_target_pairs={{0,4},{12,8},{1,5},{13,9},{2,6},{14,10},{3,7},{15,11},{16,20},{28,... | collective-permute-start | bytes 9437192 | tf_op jit(solution)/shard_map/ppermute | solution.py:63
  265.2 436.4 %all-gather.14.cloned.1.call-start = ((), (), s32[]{:S(2)}) async-start(), calls=%async_computation.4 | async-start | bytes 15728640 | tf_op jit(solution)/shard_map/all_gather | solution.py:141
  315.7 204.1 %collective-permute-start.4 = (bf16[512,3072]{1,0:T(8,128)(2,1)}, bf16[512,3072]{1,0:T(8,128)(2,1)}, u32[]{:S(2)}, u32[]{:S(2)}) collective-permute-start(bf16[512,3072]{1,0:T(8,128)(2,1)} %get-tuple-element.170), channel_id=1, source_target_pairs={{0,4},{12,8},{1,5},{13,9},{2,6},{14,10},{3,7},{15,11},{16,20},{28,... | collective-permute-start | bytes 9437192 | tf_op jit(solution)/shard_map/ppermute | solution.py:63
  370.6 143.9 %collective-permute-start.2 = (bf16[512,3072]{1,0:T(8,128)(2,1)}, bf16[512,3072]{1,0:T(8,128)(2,1)}, u32[]{:S(2)}, u32[]{:S(2)}) collective-permute-start(bf16[512,3072]{1,0:T(8,128)(2,1)} %reduce-precision_convert_fusion.27), channel_id=1, source_target_pairs={{4,8},{8,4},{5,9},{9,5},{6,10},{10,6},{7,11},{11,7},{20,24},{24,20... | collective-permute-start | bytes 9437192 | tf_op jit(solution)/shard_map/ppermute | solution.py:67
  442.0 300.7 %collective-permute-start.9 = (bf16[512,3072]{1,0:T(8,128)(2,1)}, bf16[512,3072]{1,0:T(8,128)(2,1)}, u32[]{:S(2)}, u32[]{:S(2)}) collective-permute-start(bf16[512,3072]{1,0:T(8,128)(2,1)} %get-tuple-element.184), channel_id=1, source_target_pairs={{0,4},{12,8},{1,5},{13,9},{2,6},{14,10},{3,7},{15,11},{16,20},{28,... | collective-permute-start | bytes 9437192 | tf_op jit(solution)/shard_map/ppermute | solution.py:63
  449.4 265.2 %collective-permute-start.6 = (bf16[512,3072]{1,0:T(8,128)(2,1)}, bf16[512,3072]{1,0:T(8,128)(2,1)}, u32[]{:S(2)}, u32[]{:S(2)}) collective-permute-start(bf16[512,3072]{1,0:T(8,128)(2,1)} %get-tuple-element.177), channel_id=1, source_target_pairs={{0,4},{12,8},{1,5},{13,9},{2,6},{14,10},{3,7},{15,11},{16,20},{28,... | collective-permute-start | bytes 9437192 | tf_op jit(solution)/shard_map/ppermute | solution.py:63
  518.5 72.9 %collective-permute-start.3 = (bf16[512,3072]{1,0:T(8,128)(2,1)S(1)}, bf16[512,3072]{1,0:T(8,128)(2,1)S(1)}, u32[]{:S(2)}, u32[]{:S(2)}) collective-permute-start(bf16[512,3072]{1,0:T(8,128)(2,1)S(1)} %reduce-precision_convert_fusion.25), channel_id=1, source_target_pairs={{4,0},{8,12},{5,1},{9,13},{6,2},{10,14},{7,3},{11,15},{20,16},{24,... | collective-permute-start | bytes 9437192 | tf_op jit(solution)/shard_map/ppermute | solution.py:71
  528.2 128.3 %collective-permute-start.8 = (bf16[512,3072]{1,0:T(8,128)(2,1)S(1)}, bf16[512,3072]{1,0:T(8,128)(2,1)S(1)}, u32[]{:S(2)}, u32[]{:S(2)}) collective-permute-start(bf16[512,3072]{1,0:T(8,128)(2,1)S(1)} %reduce-precision_convert_fusion.23), channel_id=1, source_target_pairs={{4,0},{8,12},{5,1},{9,13},{6,2},{10,14},{7,3},{11,15},{20,16},{24,... | collective-permute-start | bytes 9437192 | tf_op jit(solution)/shard_map/ppermute | solution.py:71
  538.3 454.7 %collective-permute-start.18 = (bf16[512,3072]{1,0:T(8,128)(2,1)}, bf16[512,3072]{1,0:T(8,128)(2,1)}, u32[]{:S(2)}, u32[]{:S(2)}) collective-permute-start(bf16[512,3072]{1,0:T(8,128)(2,1)} %get-tuple-element.218), channel_id=1, source_target_pairs={{0,4},{12,8},{1,5},{13,9},{2,6},{14,10},{3,7},{15,11},{16,20},{28,... | collective-permute-start | bytes 9437192 | tf_op jit(solution)/shard_map/ppermute | solution.py:63
  591.3 72.3 %collective-permute-start.7 = (bf16[512,3072]{1,0:T(8,128)(2,1)S(1)}, bf16[512,3072]{1,0:T(8,128)(2,1)}, u32[]{:S(2)}, u32[]{:S(2)}) collective-permute-start(bf16[512,3072]{1,0:T(8,128)(2,1)S(1)} %reduce-precision_convert_fusion.24), channel_id=1, source_target_pairs={{4,8},{8,4},{5,9},{9,5},{6,10},{10,6},{7,11},{11,7},{20,24},{24,20... | collective-permute-start | bytes 9437192 | tf_op jit(solution)/shard_map/ppermute | solution.py:67
  656.5 268.4 %collective-permute-start.15 = (bf16[512,3072]{1,0:T(8,128)(2,1)}, bf16[512,3072]{1,0:T(8,128)(2,1)}, u32[]{:S(2)}, u32[]{:S(2)}) collective-permute-start(bf16[512,3072]{1,0:T(8,128)(2,1)} %get-tuple-element.208), channel_id=1, source_target_pairs={{0,4},{12,8},{1,5},{13,9},{2,6},{14,10},{3,7},{15,11},{16,20},{28,... | collective-permute-start | bytes 9437192 | tf_op jit(solution)/shard_map/ppermute | solution.py:63
  742.7 99.9 %collective-permute-start.12 = (bf16[512,3072]{1,0:T(8,128)(2,1)}, bf16[512,3072]{1,0:T(8,128)(2,1)}, u32[]{:S(2)}, u32[]{:S(2)}) collective-permute-start(bf16[512,3072]{1,0:T(8,128)(2,1)} %get-tuple-element.198), channel_id=1, source_target_pairs={{0,4},{12,8},{1,5},{13,9},{2,6},{14,10},{3,7},{15,11},{16,20},{28,... | collective-permute-start | bytes 9437192 | tf_op jit(solution)/shard_map/ppermute | solution.py:63
  754.8 101.4 %collective-permute-start.13 = (bf16[512,3072]{1,0:T(8,128)(2,1)}, bf16[512,3072]{1,0:T(8,128)(2,1)}, u32[]{:S(2)}, u32[]{:S(2)}) collective-permute-start(bf16[512,3072]{1,0:T(8,128)(2,1)} %reduce-precision_convert_fusion.20), channel_id=1, source_target_pairs={{4,8},{8,4},{5,9},{9,5},{6,10},{10,6},{7,11},{11,7},{20,24},{24,20... | collective-permute-start | bytes 9437192 | tf_op jit(solution)/shard_map/ppermute | solution.py:67
  842.6 225.8 %collective-permute-start.21 = (bf16[512,3072]{1,0:T(8,128)(2,1)}, bf16[512,3072]{1,0:T(8,128)(2,1)}, u32[]{:S(2)}, u32[]{:S(2)}) collective-permute-start(bf16[512,3072]{1,0:T(8,128)(2,1)} %convolution_convert_fusion.11), channel_id=1, source_target_pairs={{0,4},{12,8},{1,5},{13,9},{2,6},{14,10},{3,7},{15,11},{16,20},{28,... | collective-permute-start | bytes 9437192 | tf_op jit(solution)/shard_map/ppermute | solution.py:63
  1001.3 72.9 %collective-permute-start.22 = (bf16[512,3072]{1,0:T(8,128)(2,1)}, bf16[512,3072]{1,0:T(8,128)(2,1)}, u32[]{:S(2)}, u32[]{:S(2)}) collective-permute-start(bf16[512,3072]{1,0:T(8,128)(2,1)} %reduce-precision_convert_fusion.14), channel_id=1, source_target_pairs={{4,8},{8,4},{5,9},{9,5},{6,10},{10,6},{7,11},{11,7},{20,24},{24,20... | collective-permute-start | bytes 9437192 | tf_op jit(solution)/shard_map/ppermute | solution.py:67
  1079.8 134.0 %collective-permute-start.27 = (bf16[512,3072]{1,0:T(8,128)(2,1)}, bf16[512,3072]{1,0:T(8,128)(2,1)}, u32[]{:S(2)}, u32[]{:S(2)}) collective-permute-start(bf16[512,3072]{1,0:T(8,128)(2,1)} %reduce-precision_convert_fusion.11), channel_id=1, source_target_pairs={{4,0},{8,12},{5,1},{9,13},{6,2},{10,14},{7,3},{11,15},{20,16},{24,... | collective-permute-start | bytes 9437192 | tf_op jit(solution)/shard_map/ppermute | solution.py:71
  1081.1 193.4 %collective-permute-start.23 = (bf16[512,3072]{1,0:T(8,128)(2,1)S(1)}, bf16[512,3072]{1,0:T(8,128)(2,1)}, u32[]{:S(2)}, u32[]{:S(2)}) collective-permute-start(bf16[512,3072]{1,0:T(8,128)(2,1)S(1)} %reduce-precision_convert_fusion.13), channel_id=1, source_target_pairs={{4,0},{8,12},{5,1},{9,13},{6,2},{10,14},{7,3},{11,15},{20,16},{24,... | collective-permute-start | bytes 9437192 | tf_op jit(solution)/shard_map/ppermute | solution.py:71
  1098.8 241.1 %collective-permute-start.24 = (bf16[512,3072]{1,0:T(8,128)(2,1)}, bf16[512,3072]{1,0:T(8,128)(2,1)}, u32[]{:S(2)}, u32[]{:S(2)}) collective-permute-start(bf16[512,3072]{1,0:T(8,128)(2,1)} %convolution_convert_fusion.10), channel_id=1, source_target_pairs={{0,4},{12,8},{1,5},{13,9},{2,6},{14,10},{3,7},{15,11},{16,20},{28,... | collective-permute-start | bytes 9437192 | tf_op jit(solution)/shard_map/ppermute | solution.py:63
  1169.1 194.4 %collective-permute-start.28 = (bf16[512,3072]{1,0:T(8,128)(2,1)}, bf16[512,3072]{1,0:T(8,128)(2,1)}, u32[]{:S(2)}, u32[]{:S(2)}) collective-permute-start(bf16[512,3072]{1,0:T(8,128)(2,1)} %convolution_convert_fusion.9), channel_id=1, source_target_pairs={{0,4},{12,8},{1,5},{13,9},{2,6},{14,10},{3,7},{15,11},{16,20},{28,... | collective-permute-start | bytes 9437192 | tf_op jit(solution)/shard_map/ppermute | solution.py:63
  1172.0 219.1 %collective-permute-start.31 = (bf16[512,3072]{1,0:T(8,128)(2,1)}, bf16[512,3072]{1,0:T(8,128)(2,1)}, u32[]{:S(2)}, u32[]{:S(2)}) collective-permute-start(bf16[512,3072]{1,0:T(8,128)(2,1)} %convolution_convert_fusion.8), channel_id=1, source_target_pairs={{0,4},{12,8},{1,5},{13,9},{2,6},{14,10},{3,7},{15,11},{16,20},{28,... | collective-permute-start | bytes 9437192 | tf_op jit(solution)/shard_map/ppermute | solution.py:63
  1213.8 238.5 %collective-permute-start.34 = (bf16[512,3072]{1,0:T(8,128)(2,1)}, bf16[512,3072]{1,0:T(8,128)(2,1)}, u32[]{:S(2)}, u32[]{:S(2)}) collective-permute-start(bf16[512,3072]{1,0:T(8,128)(2,1)} %convolution_convert_fusion.7), channel_id=1, source_target_pairs={{0,4},{12,8},{1,5},{13,9},{2,6},{14,10},{3,7},{15,11},{16,20},{28,... | collective-permute-start | bytes 9437192 | tf_op jit(solution)/shard_map/ppermute | solution.py:63
  1274.5 82.5 %collective-permute-start.25 = (bf16[512,3072]{1,0:T(8,128)(2,1)}, bf16[512,3072]{1,0:T(8,128)(2,1)}, u32[]{:S(2)}, u32[]{:S(2)}) collective-permute-start(bf16[512,3072]{1,0:T(8,128)(2,1)} %reduce-precision_convert_fusion.12), channel_id=1, source_target_pairs={{4,8},{8,4},{5,9},{9,5},{6,10},{10,6},{7,11},{11,7},{20,24},{24,20... | collective-permute-start | bytes 9437192 | tf_op jit(solution)/shard_map/ppermute | solution.py:67
  1339.9 188.4 %collective-permute-start.37 = (bf16[512,3072]{1,0:T(8,128)(2,1)}, bf16[512,3072]{1,0:T(8,128)(2,1)}, u32[]{:S(2)}, u32[]{:S(2)}) collective-permute-start(bf16[512,3072]{1,0:T(8,128)(2,1)} %convolution_convert_fusion.6), channel_id=1, source_target_pairs={{0,4},{12,8},{1,5},{13,9},{2,6},{14,10},{3,7},{15,11},{16,20},{28,... | collective-permute-start | bytes 9437192 | tf_op jit(solution)/shard_map/ppermute | solution.py:63
  1369.2 75.1 %collective-permute-start.32 = (bf16[512,3072]{1,0:T(8,128)(2,1)}, bf16[512,3072]{1,0:T(8,128)(2,1)}, u32[]{:S(2)}, u32[]{:S(2)}) collective-permute-start(bf16[512,3072]{1,0:T(8,128)(2,1)} %reduce-precision_convert_fusion.8), channel_id=1, source_target_pairs={{4,8},{8,4},{5,9},{9,5},{6,10},{10,6},{7,11},{11,7},{20,24},{24,20... | collective-permute-start | bytes 9437192 | tf_op jit(solution)/shard_map/ppermute | solution.py:67
  1384.1 97.8 %collective-permute-start.26 = (bf16[512,3072]{1,0:T(8,128)(2,1)S(1)}, bf16[512,3072]{1,0:T(8,128)(2,1)S(1)}, u32[]{:S(2)}, u32[]{:S(2)}) collective-permute-start(bf16[512,3072]{1,0:T(8,128)(2,1)S(1)} %reduce-precision_convert_fusion.9), channel_id=1, source_target_pairs={{4,0},{8,12},{5,1},{9,13},{6,2},{10,14},{7,3},{11,15},{20,16},{24,... | collective-permute-start | bytes 9437192 | tf_op jit(solution)/shard_map/ppermute | solution.py:71
  1391.1 239.7 %collective-permute-start.40 = (bf16[256,3072]{1,0:T(8,128)(2,1)}, bf16[256,3072]{1,0:T(8,128)(2,1)}, u32[]{:S(2)}, u32[]{:S(2)}) collective-permute-start(bf16[256,3072]{1,0:T(8,128)(2,1)} %get-tuple-element.264), channel_id=1, source_target_pairs={{0,4},{12,8},{1,5},{13,9},{2,6},{14,10},{3,7},{15,11},{16,20},{28,... | collective-permute-start | bytes 4718600 | tf_op jit(solution)/shard_map/ppermute | solution.py:63
  1444.2 77.0 %collective-permute-start.35 = (bf16[512,3072]{1,0:T(8,128)(2,1)}, bf16[512,3072]{1,0:T(8,128)(2,1)}, u32[]{:S(2)}, u32[]{:S(2)}) collective-permute-start(bf16[512,3072]{1,0:T(8,128)(2,1)} %reduce-precision_convert_fusion.6), channel_id=1, source_target_pairs={{4,8},{8,4},{5,9},{9,5},{6,10},{10,6},{7,11},{11,7},{20,24},{24,20... | collective-permute-start | bytes 9437192 | tf_op jit(solution)/shard_map/ppermute | solution.py:67
  1457.2 77.9 %collective-permute-start.38 = (bf16[512,3072]{1,0:T(8,128)(2,1)}, bf16[512,3072]{1,0:T(8,128)(2,1)}, u32[]{:S(2)}, u32[]{:S(2)}) collective-permute-start(bf16[512,3072]{1,0:T(8,128)(2,1)} %reduce-precision_convert_fusion.4), channel_id=1, source_target_pairs={{4,8},{8,4},{5,9},{9,5},{6,10},{10,6},{7,11},{11,7},{20,24},{24,20... | collective-permute-start | bytes 9437192 | tf_op jit(solution)/shard_map/ppermute | solution.py:67
  1481.9 258.2 %collective-permute-start.43 = (bf16[256,3072]{1,0:T(8,128)(2,1)}, bf16[256,3072]{1,0:T(8,128)(2,1)}, u32[]{:S(2)}, u32[]{:S(2)}) collective-permute-start(bf16[256,3072]{1,0:T(8,128)(2,1)} %get-tuple-element.269), channel_id=1, source_target_pairs={{0,4},{12,8},{1,5},{13,9},{2,6},{14,10},{3,7},{15,11},{16,20},{28,... | collective-permute-start | bytes 4718600 | tf_op jit(solution)/shard_map/ppermute | solution.py:63
  1521.2 115.5 %collective-permute-start.30 = (bf16[512,3072]{1,0:T(8,128)(2,1)S(1)}, bf16[512,3072]{1,0:T(8,128)(2,1)S(1)}, u32[]{:S(2)}, u32[]{:S(2)}) collective-permute-start(bf16[512,3072]{1,0:T(8,128)(2,1)S(1)} %copy-done.21), channel_id=1, source_target_pairs={{4,0},{8,12},{5,1},{9,13},{6,2},{10,14},{7,3},{11,15},{20,16},{24,... | collective-permute-start | bytes 9437192 | tf_op jit(solution)/shard_map/ppermute | solution.py:71
  1528.2 155.2 %collective-permute-start.33 = (bf16[512,3072]{1,0:T(8,128)(2,1)}, bf16[512,3072]{1,0:T(8,128)(2,1)}, u32[]{:S(2)}, u32[]{:S(2)}) collective-permute-start(bf16[512,3072]{1,0:T(8,128)(2,1)} %reduce-precision_convert_fusion.5), channel_id=1, source_target_pairs={{4,0},{8,12},{5,1},{9,13},{6,2},{10,14},{7,3},{11,15},{20,16},{24,... | collective-permute-start | bytes 9437192 | tf_op jit(solution)/shard_map/ppermute | solution.py:71
  1535.1 210.9 %collective-permute-start.46 = (bf16[128,3072]{1,0:T(8,128)(2,1)}, bf16[128,3072]{1,0:T(8,128)(2,1)}, u32[]{:S(2)}, u32[]{:S(2)}) collective-permute-start(bf16[128,3072]{1,0:T(8,128)(2,1)} %get-tuple-element.273), channel_id=1, source_target_pairs={{0,4},{12,8},{1,5},{13,9},{2,6},{14,10},{3,7},{15,11},{16,20},{28,... | collective-permute-start | bytes 2359304 | tf_op jit(solution)/shard_map/ppermute | solution.py:63
  1683.4 119.2 %collective-permute-start.49 = (bf16[128,3072]{1,0:T(8,128)(2,1)}, bf16[128,3072]{1,0:T(8,128)(2,1)}, u32[]{:S(2)}, u32[]{:S(2)}) collective-permute-start(bf16[128,3072]{1,0:T(8,128)(2,1)} %get-tuple-element.277), channel_id=1, source_target_pairs={{0,4},{12,8},{1,5},{13,9},{2,6},{14,10},{3,7},{15,11},{16,20},{28,... | collective-permute-start | bytes 2359304 | tf_op jit(solution)/shard_map/ppermute | solution.py:63
  1690.4 100.2 %collective-permute-start.36 = (bf16[512,3072]{1,0:T(8,128)(2,1)}, bf16[512,3072]{1,0:T(8,128)(2,1)S(1)}, u32[]{:S(2)}, u32[]{:S(2)}) collective-permute-start(bf16[512,3072]{1,0:T(8,128)(2,1)} %reduce-precision_convert_fusion.3), channel_id=1, source_target_pairs={{4,0},{8,12},{5,1},{9,13},{6,2},{10,14},{7,3},{11,15},{20,16},{24,... | collective-permute-start | bytes 9437192 | tf_op jit(solution)/shard_map/ppermute | solution.py:71
  1695.3 111.8 %collective-permute-start.52 = (bf16[128,3072]{1,0:T(8,128)(2,1)}, bf16[128,3072]{1,0:T(8,128)(2,1)}, u32[]{:S(2)}, u32[]{:S(2)}) collective-permute-start(bf16[128,3072]{1,0:T(8,128)(2,1)} %get-tuple-element.281), channel_id=1, source_target_pairs={{0,4},{12,8},{1,5},{13,9},{2,6},{14,10},{3,7},{15,11},{16,20},{28,... | collective-permute-start | bytes 2359304 | tf_op jit(solution)/shard_map/ppermute | solution.py:63
  1740.2 73.3 %collective-permute-start.57 = (bf16[128,3072]{1,0:T(8,128)(2,1)}, bf16[128,3072]{1,0:T(8,128)(2,1)}, u32[]{:S(2)}, u32[]{:S(2)}) collective-permute-start(bf16[128,3072]{1,0:T(8,128)(2,1)} %get-tuple-element.286), channel_id=1, source_target_pairs={{0,4},{12,8},{1,5},{13,9},{2,6},{14,10},{3,7},{15,11},{16,20},{28,... | collective-permute-start | bytes 2359304 | tf_op jit(solution)/shard_map/ppermute | solution.py:63
  1792.3 73.2 %collective-permute-start.39 = (bf16[512,3072]{1,0:T(8,128)(2,1)}, bf16[512,3072]{1,0:T(8,128)(2,1)}, u32[]{:S(2)}, u32[]{:S(2)}) collective-permute-start(bf16[512,3072]{1,0:T(8,128)(2,1)} %reduce-precision_convert_fusion.1), channel_id=1, source_target_pairs={{4,0},{8,12},{5,1},{9,13},{6,2},{10,14},{7,3},{11,15},{20,16},{24,... | collective-permute-start | bytes 9437192 | tf_op jit(solution)/shard_map/ppermute | solution.py:71
  1802.7 130.2 %collective-permute-start.42 = (bf16[512,3072]{1,0:T(8,128)(2,1)}, bf16[512,3072]{1,0:T(8,128)(2,1)}, u32[]{:S(2)}, u32[]{:S(2)}) collective-permute-start(bf16[512,3072]{1,0:T(8,128)(2,1)} %reduce-precision_convert_fusion), channel_id=1, source_target_pairs={{4,0},{8,12},{5,1},{9,13},{6,2},{10,14},{7,3},{11,15},{20,16},{24,... | collective-permute-start | bytes 9437192 | tf_op jit(solution)/shard_map/ppermute | solution.py:71
  1807.1 159.5 %collective-permute-start.45 = (bf16[256,3072]{1,0:T(8,128)(2,1)}, bf16[256,3072]{1,0:T(8,128)(2,1)}, u32[]{:S(2)}, u32[]{:S(2)}) collective-permute-start(bf16[256,3072]{1,0:T(8,128)(2,1)} %reduce-precision_convert_fusion.29), channel_id=1, source_target_pairs={{4,0},{8,12},{5,1},{9,13},{6,2},{10,14},{7,3},{11,15},{20,16},{24,... | collective-permute-start | bytes 4718600 | tf_op jit(solution)/shard_map/ppermute | solution.py:71
  1870.1 130.2 %collective-permute-start.48 = (bf16[256,3072]{1,0:T(8,128)(2,1)}, bf16[256,3072]{1,0:T(8,128)(2,1)}, u32[]{:S(2)}, u32[]{:S(2)}) collective-permute-start(bf16[256,3072]{1,0:T(8,128)(2,1)} %reduce-precision_convert_fusion.28), channel_id=1, source_target_pairs={{4,0},{8,12},{5,1},{9,13},{6,2},{10,14},{7,3},{11,15},{20,16},{24,... | collective-permute-start | bytes 4718600 | tf_op jit(solution)/shard_map/ppermute | solution.py:71
  1871.4 145.8 %collective-permute-start.51 = (bf16[128,3072]{1,0:T(8,128)(2,1)}, bf16[128,3072]{1,0:T(8,128)(2,1)}, u32[]{:S(2)}, u32[]{:S(2)}) collective-permute-start(bf16[128,3072]{1,0:T(8,128)(2,1)} %reduce-precision_convert_fusion.37), channel_id=1, source_target_pairs={{4,0},{8,12},{5,1},{9,13},{6,2},{10,14},{7,3},{11,15},{20,16},{24,... | collective-permute-start | bytes 2359304 | tf_op jit(solution)/shard_map/ppermute | solution.py:71
  1875.2 158.8 %collective-permute-start.54 = (bf16[128,3072]{1,0:T(8,128)(2,1)}, bf16[128,3072]{1,0:T(8,128)(2,1)}, u32[]{:S(2)}, u32[]{:S(2)}) collective-permute-start(bf16[128,3072]{1,0:T(8,128)(2,1)} %reduce-precision_convert_fusion.35), channel_id=1, source_target_pairs={{4,0},{8,12},{5,1},{9,13},{6,2},{10,14},{7,3},{11,15},{20,16},{24,... | collective-permute-start | bytes 2359304 | tf_op jit(solution)/shard_map/ppermute | solution.py:71
  1932.9 115.4 %collective-permute-start.56 = (bf16[128,3072]{1,0:T(8,128)(2,1)}, bf16[128,3072]{1,0:T(8,128)(2,1)}, u32[]{:S(2)}, u32[]{:S(2)}) collective-permute-start(bf16[128,3072]{1,0:T(8,128)(2,1)} %reduce-precision_convert_fusion.34), channel_id=1, source_target_pairs={{4,0},{8,12},{5,1},{9,13},{6,2},{10,14},{7,3},{11,15},{20,16},{24,... | collective-permute-start | bytes 2359304 | tf_op jit(solution)/shard_map/ppermute | solution.py:71
  1966.6 90.0 %collective-permute-start.59 = (bf16[128,3072]{1,0:T(8,128)(2,1)}, bf16[128,3072]{1,0:T(8,128)(2,1)S(1)}, u32[]{:S(2)}, u32[]{:S(2)}) collective-permute-start(bf16[128,3072]{1,0:T(8,128)(2,1)} %reduce-precision_convert_fusion.32), channel_id=1, source_target_pairs={{4,0},{8,12},{5,1},{9,13},{6,2},{10,14},{7,3},{11,15},{20,16},{24,... | collective-permute-start | bytes 2359304 | tf_op jit(solution)/shard_map/ppermute | solution.py:71
  (126 other events, 3187.1 us)
Sparse Core Ops, SparseCore 0:
  9.6 58.0 all-gather.5
  69.2 37.4 all-gather.7
  112.7 82.0 all-gather.11
  265.4 81.4 all-gather.9
  484.1 80.4 all-gather.13

commit v2 on v1

--- a/solution.py
+++ b/solution.py
@@ -39,6 +39,7 @@
 
 
 ROW_SPLIT = 2
+MLP_LATER = 2
 
 
 def split_qkv(qkv_cols, kv_local, head_dim):
@@ -94,10 +95,9 @@
     return items
 
 
-def attention(x_prompt, length, qkv_cols, o_rows, g_attn, cos_tab, sin_tab, kv_local, head_dim):
-    seq_len = x_prompt.shape[0]
-    group_size = qkv_cols.shape[1] // (kv_local * head_dim) - 2
-    qkv_act = dot_f32(rms_norm(x_prompt, g_attn), qkv_cols).astype(jnp.bfloat16)
+def attention(qkv_act, length, o_rows, cos_tab, sin_tab, kv_local, head_dim):
+    seq_len = qkv_act.shape[0]
+    group_size = qkv_act.shape[1] // (kv_local * head_dim) - 2
     qkv_act = qkv_act.reshape(seq_len, kv_local, group_size + 2, head_dim)
     q_rot = apply_rope(qkv_act[:, :, :group_size, :].astype(jnp.float32), cos_tab[:, None, None, :], sin_tab[:, None, None, :]).astype(jnp.bfloat16)
     k_rot = apply_rope(qkv_act[:, :, group_size, :].astype(jnp.float32), cos_tab[:, None, :], sin_tab[:, None, :]).astype(jnp.bfloat16)
@@ -134,10 +134,11 @@
         qkv_cols = lax.all_gather(w_qkv, 'tpb', axis=1, tiled=True)
         w_o, qkv_cols = lax.optimization_barrier((w_o, qkv_cols))
         o_rows = lax.all_gather(w_o, 'tpb', axis=0, tiled=True)
-        w_gate_up, o_rows = lax.optimization_barrier((w_gate_up, o_rows))
+        qkv_first = dot_f32(rms_norm(x_loc[0], g_attn), qkv_cols).astype(jnp.bfloat16)
+        w_gate_up, qkv_first = tie((w_gate_up, qkv_first))
         w_gate = lax.all_gather(w_gate_up[:, :ff_block], 'tpb', axis=1, tiled=True)
         w_up = lax.all_gather(w_gate_up[:, ff_block:], 'tpb', axis=1, tiled=True)
-        w_down, w_up = lax.optimization_barrier((w_down, w_up))
+        w_down, qkv_first = tie((w_down, qkv_first))
         down_rows = lax.all_gather(w_down, 'tpb', axis=0, tiled=True)
         cos_tab, sin_tab = rope_tables(seq_len, head_dim)
         layer_out = jnp.zeros_like(x_loc)
@@ -149,7 +150,8 @@
         n_items = len(items)
         first, total, mlp_part, hidden = {}, {}, {}, {}
         waiting, settled = {'o': o_rows, 'gate': w_gate, 'up': w_up, 'down': down_rows}, {}
-        x_prompt = {b: x_loc[b] for b in range(batch_loc)}
+        cols_of = {b: qkv_cols for b in range(batch_loc)}
+        summed = {}
         attn_part = None
         for t in range(n_items + 2):
             if t < n_items:
@@ -157,9 +159,12 @@
                 if kind == 'attn':
                     b, r = chunks[c]
                     if r == 0:
-                        attn_part, k_rot, values = attention(x_prompt[b], len_loc[b], qkv_cols, o_rows, g_attn, cos_tab, sin_tab, kv_local, head_dim)
+                        qkv_act = qkv_first
+                        if b:
+                            qkv_act = dot_f32(rms_norm(x_loc[b], g_attn), cols_of[b]).astype(jnp.bfloat16)
+                        attn_part, k_rot, values = attention(qkv_act, len_loc[b], o_rows, cos_tab, sin_tab, kv_local, head_dim)
                         if b + 1 < batch_loc:
-                            x_prompt[b + 1], attn_part, k_rot, values = tie((x_prompt[b + 1], attn_part, k_rot, values))
+                            cols_of[b + 1], attn_part, k_rot, values = tie((cols_of[b + 1], attn_part, k_rot, values))
                         k_new.append(k_rot)
                         v_new.append(values)
                     part = attn_part[r:r + rows]
@@ -169,34 +174,41 @@
             if t >= 1 and t - 1 < n_items:
                 if t < n_items:
                     if t + 1 < batch_loc:
-                        part, first[t - 1], x_prompt[t + 1] = tie((part, first[t - 1], x_prompt[t + 1]))
+                        part, first[t - 1], cols_of[t + 1] = tie((part, first[t - 1], cols_of[t + 1]))
                     else:
                         part, first[t - 1] = tie((part, first[t - 1]))
                 crossed = across(first[t - 1], 'tpa')
                 total_next = add_bf16(first[t - 1], crossed)
-            if t >= 2:
+            if 2 <= t < n_items + 2:
                 if t < n_items:
                     part, total[t - 2] = tie((part, total[t - 2]))
                 kind, c, start, size = items[t - 2]
                 b, r = chunks[c]
-                summed = outward(total[t - 2], 'tpa')
+                out = outward(total[t - 2], 'tpa')
                 if kind == 'attn':
-                    x_rows, summed = tie((x_loc[b, r:r + rows], summed))
-                    hidden[c] = residual(x_rows, summed)
-                    mlp_part[c] = mlp(hidden[c], w_gate, w_up, down_rows, g_mlp)
+                    summed[c] = out
                 else:
-                    piece = residual(hidden[c][start:start + size], summed)
+                    piece = residual(hidden[c][start:start + size], out)
                     layer_out = lax.dynamic_update_slice(layer_out, piece[None], (b, r + start, 0))
-            if 3 <= t < n_items and items[t - 3][0] == 'attn':
-                c = items[t - 3][1]
+            c = t - 2 - MLP_LATER
+            if c in summed:
+                b, r = chunks[c]
+                if c:
+                    summed[c], mlp_part[c - 1] = tie((summed[c], mlp_part[c - 1]))
+                hidden[c] = residual(x_loc[b, r:r + rows], summed[c])
+                mlp_part[c] = mlp(hidden[c], w_gate, w_up, down_rows, g_mlp)
+            c = t - 3 - MLP_LATER
+            if c in mlp_part:
                 part, mlp_part[c] = tie((part, mlp_part[c]))
-                name = {2: 'o', 3: 'gate', 4: 'up', 5: 'down'}.get(c)
+            if t < n_items:
+                for name in list(settled):
+                    part, settled[name] = tie((part, settled[name]))
+                name = {n_chunks + 3: 'o', n_chunks + 4: 'gate', n_chunks + 5: 'up', n_chunks + 6: 'down'}.get(t)
                 if name:
-                    waiting[name], mlp_part[c] = tie((waiting[name], mlp_part[c]))
+                    waiting[name], total[t - 2] = tie((waiting[name], total[t - 2]))
                     settled[name] = settle(waiting[name])
-                    part, settled[name] = tie((part, settled[name]))
-                if c == n_chunks - 3:
-                    qkv_cols, mlp_part[c] = tie((qkv_cols, mlp_part[c]))
+                if t == n_chunks + 2:
+                    qkv_cols, total[t - 2] = tie((qkv_cols, total[t - 2]))
             if t < n_items:
                 first[t] = add_bf16(part, got)
             if t >= 1 and t - 1 < n_items:

time: 2090 us -> 1880 us (0.90)
  waiting for transfers between devices: 711 us -> 578 us
  starting transfers between devices: 408 us -> 338 us
  local copies, waits for them, and re-layouts: 165 us -> 114 us
  matrix products: 434 us -> 469 us
    ppermute x20, waiting for transfers between devices: 573 us -> 347 us  [outward(): got = lax.ppermute(total, axis, [(1, 0), (2, 3)])]
    ppermute x20, waiting for transfers between devices: 46.9 us -> 170 us  [inward(): return lax.ppermute(part, axis, [(0, 1), (3, 2)])]
    ppermute x20, starting transfers between devices: 341 us -> 268 us  [inward(): return lax.ppermute(part, axis, [(0, 1), (3, 2)])]
    dot_general x32, matrix products: 323 us -> 362 us  [dot_f32(): return jnp.dot(lhs, rhs, preferred_element_type=jnp.float32)]
    squeeze x2 -> x0, local copies, waits for them, and re-layouts: 33.8 us -> none  [the longest x1 17.9 us: one_layer(): x_rows, summed = tie((x_loc[b, r:r + rows], summed))]
    all_gather x1, waiting for transfers between devices: 31 us -> 0.02 us  [one_layer(): o_rows = lax.all_gather(w_o, 'tpb', axis=0, tiled=True)]
    unnamed x235 -> x155, local copies, waits for them, and re-layouts: 57.9 us -> 34.7 us
  transfers between devices with their start and end apart: 65 -> 65, of which waited for: 22 -> 19; matrix products, arithmetic and copies ran while one was open for 41% -> 48% of each run, Pallas kernels for 2% -> 2%
where the time goes in v2:
time: 1880 us; the launch traced here: 1870 us
  waiting for transfers between devices  578 us (31%)
  matrix products  469 us (25%)
  starting transfers between devices  338 us (18%)
  other arithmetic  312 us (17%)
  local copies, waits for them, and re-layouts  114 us (6%)
  Pallas kernels  43.4 us (2%)
    dot_general x32, matrix products, dot_f32(): return jnp.dot(lhs, rhs, preferred_element_type=jnp.float32)  362 us
    ppermute x20, waiting for transfers between devices, outward(): got = lax.ppermute(total, axis, [(1, 0), (2, 3)])  347 us
    ppermute x20, starting transfers between devices, inward(): return lax.ppermute(part, axis, [(0, 1), (3, 2)])  268 us
    convert_element_type x40, other arithmetic, add_bf16(): lax.reduce_precision(a.astype(jnp.float32) + b.astype(jnp.float32), 8, 7)  171 us
    ppermute x20, waiting for transfers between devices, inward(): return lax.ppermute(part, axis, [(0, 1), (3, 2)])  170 us
    sub x4, matrix products, attention(): attn_prob = jax.nn.softmax(scores, axis=-1).astype(jnp.bfloat16)  65.8 us
    all_gather x1, waiting for transfers between devices, one_layer(): qkv_cols = lax.all_gather(w_qkv, 'tpb', axis=1, tiled=True)  59.6 us
    pallas_call x4, Pallas kernels, settle(): pl.pallas_call(body, grid=(rows // min(rows, 256),), in_specs=[block], ou...  43.4 us
  transfers between devices with their start and end apart: 65, of which 19 were waited for; matrix products, arithmetic and copies ran while one was open for 48% of the time, Pallas kernels for 2%

profile of v2, /device:TPU:0, one launch (start us, length us, event | category | flops | bytes accessed | tf_op | source)
XLA Modules:
  0.0 1870.0 jit_solution(3629945456966738991)
XLA Ops:
  8.0 59.6 %all-gather.6.cloned.1.call-done = bf16[3072,1280]{0,1:T(8,128)(2,1)} async-done(((bf16[3072,320]{0,1:T(8,128)(2,1)}), bf16[3072,1280]{0,1:T(8,128)(2,1)}) %all-gather.6.cloned.1.call-update) | async-done | bytes 7864336 | tf_op jit(solution)/shard_map/all_gather | solution.py:134
  67.7 12.3 fusion.14
  80.0 12.0 fusion.142
  128.8 15.8 fusion.282
  164.7 14.0 fusion.145
  211.0 16.4 fusion.287
  247.2 17.4 collective-permute-done
  270.4 14.3 fusion.151
  299.5 31.7 %collective-permute-done.1 = bf16[512,3072]{1,0:T(8,128)(2,1)} collective-permute-done((bf16[512,3072]{1,0:T(8,128)(2,1)}, bf16[512,3072]{1,0:T(8,128)(2,1)}, u32[]{:S(2)}, u32[]{:S(2)}) %collective-permute-start.1) | collective-permute-done | bytes 3145760 | tf_op jit(solution)/shard_map/ppermute | solution.py:64
  346.1 16.2 fusion.292
  381.9 14.2 fusion.148
  434.8 17.3 fusion.297
  491.1 119.2 %collective-permute-done.6 = bf16[512,3072]{1,0:T(8,128)(2,1)} collective-permute-done((bf16[512,3072]{1,0:T(8,128)(2,1)S(1)}, bf16[512,3072]{1,0:T(8,128)(2,1)}, u32[]{:S(2)}, u32[]{:S(2)}) %collective-permute-start.6) | collective-permute-done | bytes 3145760 | tf_op jit(solution)/shard_map/ppermute | solution.py:64
  663.2 29.0 %collective-permute-start.17 = (bf16[512,3072]{1,0:T(8,128)(2,1)}, bf16[512,3072]{1,0:T(8,128)(2,1)}, u32[]{:S(2)}, u32[]{:S(2)}) collective-permute-start(bf16[512,3072]{1,0:T(8,128)(2,1)} %get-tuple-element.238), channel_id=1, source_target_pairs={{0,4},{12,8},{1,5},{13,9},{2,6},{14,10},{3,7},{15,11},{16,20},{28,... | collective-permute-start | bytes 9437192 | tf_op jit(solution)/shard_map/ppermute | solution.py:64
  708.6 58.5 %collective-permute-done.10 = bf16[512,3072]{1,0:T(8,128)(2,1)S(1)} collective-permute-done((bf16[512,3072]{1,0:T(8,128)(2,1)S(1)}, bf16[512,3072]{1,0:T(8,128)(2,1)S(1)}, u32[]{:S(2)}, u32[]{:S(2)}) %collective-permute-start.10) | collective-permute-done | bytes 3145760 | tf_op jit(solution)/shard_map/ppermute | solution.py:72
  770.4 11.1 convolution_convert_fusion.27
  781.4 11.3 fusion.141
  792.8 13.0 convolution_convert_fusion.11
  834.6 10.9 convolution_convert_fusion.10
  877.0 26.8 %collective-permute-done.16 = bf16[512,3072]{1,0:T(8,128)(2,1)} collective-permute-done((bf16[512,3072]{1,0:T(8,128)(2,1)}, bf16[512,3072]{1,0:T(8,128)(2,1)}, u32[]{:S(2)}, u32[]{:S(2)}) %collective-permute-start.16) | collective-permute-done | bytes 3145760 | tf_op jit(solution)/shard_map/ppermute | solution.py:72
  907.6 11.0 convolution_convert_fusion.22
  918.6 11.8 fusion.139
  930.4 12.9 convolution_convert_fusion.9
  950.4 11.9 convolution_convert_fusion.20
  962.3 11.6 fusion.138
  973.9 13.0 convolution_convert_fusion.8
  1054.8 11.6 fusion.137
  1066.5 12.9 convolution_convert_fusion.7
  1122.5 11.6 fusion.136
  1134.2 13.0 convolution_convert_fusion.6
  1169.6 11.0 convolution_convert_fusion.14
  1180.6 11.6 fusion.135
  1213.6 13.1 convolution_convert_fusion.5
  1329.4 13.2 shard_map.178
  1346.3 26.1 %collective-permute-start.43 = (bf16[256,3072]{1,0:T(8,128)(2,1)}, bf16[256,3072]{1,0:T(8,128)(2,1)}, u32[]{:S(2)}, u32[]{:S(2)}) collective-permute-start(bf16[256,3072]{1,0:T(8,128)(2,1)} %get-tuple-element.311), channel_id=1, source_target_pairs={{0,4},{12,8},{1,5},{13,9},{2,6},{14,10},{3,7},{15,11},{16,20},{28,... | collective-permute-start | bytes 4718600 | tf_op jit(solution)/shard_map/ppermute | solution.py:64
  1384.0 13.2 shard_map.179
  1397.2 33.5 %collective-permute-start.46 = (bf16[128,3072]{1,0:T(8,128)(2,1)}, bf16[128,3072]{1,0:T(8,128)(2,1)}, u32[]{:S(2)}, u32[]{:S(2)}) collective-permute-start(bf16[128,3072]{1,0:T(8,128)(2,1)} %get-tuple-element.323), channel_id=1, source_target_pairs={{0,4},{12,8},{1,5},{13,9},{2,6},{14,10},{3,7},{15,11},{16,20},{28,... | collective-permute-start | bytes 2359304 | tf_op jit(solution)/shard_map/ppermute | solution.py:64
  1449.7 11.6 shard_map.180
  1474.2 65.1 %collective-permute-start.52 = (bf16[128,3072]{1,0:T(8,128)(2,1)S(1)}, bf16[128,3072]{1,0:T(8,128)(2,1)}, u32[]{:S(2)}, u32[]{:S(2)}) collective-permute-start(bf16[128,3072]{1,0:T(8,128)(2,1)S(1)} %copy-done.30), channel_id=1, source_target_pairs={{0,4},{12,8},{1,5},{13,9},{2,6},{14,10},{3,7},{15,11},{16,20},{28,... | collective-permute-start | bytes 2359304 | tf_op jit(solution)/shard_map/ppermute | solution.py:64
  1551.0 51.5 %collective-permute-done.36 = bf16[512,3072]{1,0:T(8,128)(2,1)S(1)} collective-permute-done((bf16[512,3072]{1,0:T(8,128)(2,1)S(1)}, bf16[512,3072]{1,0:T(8,128)(2,1)S(1)}, u32[]{:S(2)}, u32[]{:S(2)}) %collective-permute-start.36) | collective-permute-done | bytes 3145760 | tf_op jit(solution)/shard_map/ppermute | solution.py:72
  1607.7 14.0 collective-permute-start.57
  1632.2 37.8 %collective-permute-done.39 = bf16[512,3072]{1,0:T(8,128)(2,1)S(1)} collective-permute-done((bf16[512,3072]{1,0:T(8,128)(2,1)S(1)}, bf16[512,3072]{1,0:T(8,128)(2,1)S(1)}, u32[]{:S(2)}, u32[]{:S(2)}) %collective-permute-start.39) | collective-permute-done | bytes 3145760 | tf_op jit(solution)/shard_map/ppermute | solution.py:72
  1683.4 54.0 %collective-permute-done.42 = bf16[512,3072]{1,0:T(8,128)(2,1)S(1)} collective-permute-done((bf16[512,3072]{1,0:T(8,128)(2,1)S(1)}, bf16[512,3072]{1,0:T(8,128)(2,1)S(1)}, u32[]{:S(2)}, u32[]{:S(2)}) %collective-permute-start.42) | collective-permute-done | bytes 3145760 | tf_op jit(solution)/shard_map/ppermute | solution.py:72
  1743.1 28.0 %collective-permute-done.45 = bf16[256,3072]{1,0:T(8,128)(2,1)S(1)} collective-permute-done((bf16[256,3072]{1,0:T(8,128)(2,1)S(1)}, bf16[256,3072]{1,0:T(8,128)(2,1)S(1)}, u32[]{:S(2)}, u32[]{:S(2)}) %collective-permute-start.45) | collective-permute-done | bytes 1572896 | tf_op jit(solution)/shard_map/ppermute | solution.py:72
  1774.3 30.5 %collective-permute-done.48 = bf16[256,3072]{1,0:T(8,128)(2,1)S(1)} collective-permute-done((bf16[256,3072]{1,0:T(8,128)(2,1)S(1)}, bf16[256,3072]{1,0:T(8,128)(2,1)S(1)}, u32[]{:S(2)}, u32[]{:S(2)}) %collective-permute-start.48) | collective-permute-done | bytes 1572896 | tf_op jit(solution)/shard_map/ppermute | solution.py:72
  1806.7 14.9 collective-permute-done.51
  1822.9 15.6 collective-permute-done.54
  1839.7 13.8 collective-permute-done.56
  (426 shorter events, 753.6 us)
Async XLA Ops:
  7.9 147.1 %all-gather.8.cloned.1.call-start = ((), (), s32[]{:S(2)}) async-start(), calls=%async_computation.1 | async-start | bytes 5898240 | tf_op jit(solution)/shard_map/all_gather | solution.py:136
  67.6 702.8 %all-gather.10.cloned.1.call-start = ((), (), s32[]{:S(2)}) async-start(), calls=%async_computation.2 | async-start | bytes 15728640 | tf_op jit(solution)/shard_map/all_gather | solution.py:139
  95.2 686.2 %all-gather.12.cloned.1.call-start = ((), (), s32[]{:S(2)}) async-start(), calls=%async_computation.3 | async-start | bytes 15728640 | tf_op jit(solution)/shard_map/all_gather | solution.py:140
  95.8 697.0 %all-gather.14.cloned.1.call-start = ((), (), s32[]{:S(2)}) async-start(), calls=%async_computation.4 | async-start | bytes 15728640 | tf_op jit(solution)/shard_map/all_gather | solution.py:142
  207.7 123.5 %collective-permute-start.1 = (bf16[512,3072]{1,0:T(8,128)(2,1)}, bf16[512,3072]{1,0:T(8,128)(2,1)}, u32[]{:S(2)}, u32[]{:S(2)}) collective-permute-start(bf16[512,3072]{1,0:T(8,128)(2,1)} %get-tuple-element.199), channel_id=1, source_target_pairs={{0,4},{12,8},{1,5},{13,9},{2,6},{14,10},{3,7},{15,11},{16,20},{28,... | collective-permute-start | bytes 9437192 | tf_op jit(solution)/shard_map/ppermute | solution.py:64
  426.3 224.6 %collective-permute-start.8 = (bf16[512,3072]{1,0:T(8,128)(2,1)}, bf16[512,3072]{1,0:T(8,128)(2,1)}, u32[]{:S(2)}, u32[]{:S(2)}) collective-permute-start(bf16[512,3072]{1,0:T(8,128)(2,1)} %get-tuple-element.213), channel_id=1, source_target_pairs={{0,4},{12,8},{1,5},{13,9},{2,6},{14,10},{3,7},{15,11},{16,20},{28,... | collective-permute-start | bytes 9437192 | tf_op jit(solution)/shard_map/ppermute | solution.py:64
  429.5 180.8 %collective-permute-start.6 = (bf16[512,3072]{1,0:T(8,128)(2,1)S(1)}, bf16[512,3072]{1,0:T(8,128)(2,1)}, u32[]{:S(2)}, u32[]{:S(2)}) collective-permute-start(bf16[512,3072]{1,0:T(8,128)(2,1)S(1)} %copy-done.20), channel_id=1, source_target_pairs={{0,4},{12,8},{1,5},{13,9},{2,6},{14,10},{3,7},{15,11},{16,20},{28,... | collective-permute-start | bytes 9437192 | tf_op jit(solution)/shard_map/ppermute | solution.py:64
  482.9 161.1 %collective-permute-start.7 = (bf16[512,3072]{1,0:T(8,128)(2,1)}, bf16[512,3072]{1,0:T(8,128)(2,1)}, u32[]{:S(2)}, u32[]{:S(2)}) collective-permute-start(bf16[512,3072]{1,0:T(8,128)(2,1)} %reduce-precision_convert_fusion.24), channel_id=1, source_target_pairs={{4,8},{8,4},{5,9},{9,5},{6,10},{10,6},{7,11},{11,7},{20,24},{24,20... | collective-permute-start | bytes 9437192 | tf_op jit(solution)/shard_map/ppermute | solution.py:68
  620.5 247.2 %collective-permute-start.14 = (bf16[512,3072]{1,0:T(8,128)(2,1)}, bf16[512,3072]{1,0:T(8,128)(2,1)}, u32[]{:S(2)}, u32[]{:S(2)}) collective-permute-start(bf16[512,3072]{1,0:T(8,128)(2,1)} %get-tuple-element.228), channel_id=1, source_target_pairs={{0,4},{12,8},{1,5},{13,9},{2,6},{14,10},{3,7},{15,11},{16,20},{28,... | collective-permute-start | bytes 9437192 | tf_op jit(solution)/shard_map/ppermute | solution.py:64
  644.0 123.1 %collective-permute-start.10 = (bf16[512,3072]{1,0:T(8,128)(2,1)S(1)}, bf16[512,3072]{1,0:T(8,128)(2,1)S(1)}, u32[]{:S(2)}, u32[]{:S(2)}) collective-permute-start(bf16[512,3072]{1,0:T(8,128)(2,1)S(1)} %copy-done.24), channel_id=1, source_target_pairs={{4,0},{8,12},{5,1},{9,13},{6,2},{10,14},{7,3},{11,15},{20,16},{24,... | collective-permute-start | bytes 9437192 | tf_op jit(solution)/shard_map/ppermute | solution.py:72
  650.9 176.6 %collective-permute-start.11 = (bf16[512,3072]{1,0:T(8,128)(2,1)}, bf16[512,3072]{1,0:T(8,128)(2,1)}, u32[]{:S(2)}, u32[]{:S(2)}) collective-permute-start(bf16[512,3072]{1,0:T(8,128)(2,1)} %get-tuple-element.221), channel_id=1, source_target_pairs={{0,4},{12,8},{1,5},{13,9},{2,6},{14,10},{3,7},{15,11},{16,20},{28,... | collective-permute-start | bytes 9437192 | tf_op jit(solution)/shard_map/ppermute | solution.py:64
  663.2 337.2 %collective-permute-start.17 = (bf16[512,3072]{1,0:T(8,128)(2,1)}, bf16[512,3072]{1,0:T(8,128)(2,1)}, u32[]{:S(2)}, u32[]{:S(2)}) collective-permute-start(bf16[512,3072]{1,0:T(8,128)(2,1)} %get-tuple-element.238), channel_id=1, source_target_pairs={{0,4},{12,8},{1,5},{13,9},{2,6},{14,10},{3,7},{15,11},{16,20},{28,... | collective-permute-start | bytes 9437192 | tf_op jit(solution)/shard_map/ppermute | solution.py:64
  702.8 142.8 %collective-permute-start.12 = (bf16[512,3072]{1,0:T(8,128)(2,1)}, bf16[512,3072]{1,0:T(8,128)(2,1)}, u32[]{:S(2)}, u32[]{:S(2)}) collective-permute-start(bf16[512,3072]{1,0:T(8,128)(2,1)} %reduce-precision_convert_fusion.20), channel_id=1, source_target_pairs={{4,8},{8,4},{5,9},{9,5},{6,10},{10,6},{7,11},{11,7},{20,24},{24,20... | collective-permute-start | bytes 9437192 | tf_op jit(solution)/shard_map/ppermute | solution.py:68
  767.1 86.6 %collective-permute-start.13 = (bf16[512,3072]{1,0:T(8,128)(2,1)}, bf16[512,3072]{1,0:T(8,128)(2,1)}, u32[]{:S(2)}, u32[]{:S(2)}) collective-permute-start(bf16[512,3072]{1,0:T(8,128)(2,1)} %reduce-precision_convert_fusion.21), channel_id=1, source_target_pairs={{4,0},{8,12},{5,1},{9,13},{6,2},{10,14},{7,3},{11,15},{20,16},{24,... | collective-permute-start | bytes 9437192 | tf_op jit(solution)/shard_map/ppermute | solution.py:72
  827.5 76.2 %collective-permute-start.16 = (bf16[512,3072]{1,0:T(8,128)(2,1)}, bf16[512,3072]{1,0:T(8,128)(2,1)}, u32[]{:S(2)}, u32[]{:S(2)}) collective-permute-start(bf16[512,3072]{1,0:T(8,128)(2,1)} %reduce-precision_convert_fusion.19), channel_id=1, source_target_pairs={{4,0},{8,12},{5,1},{9,13},{6,2},{10,14},{7,3},{11,15},{20,16},{24,... | collective-permute-start | bytes 9437192 | tf_op jit(solution)/shard_map/ppermute | solution.py:72
  845.6 141.4 %collective-permute-start.15 = (bf16[512,3072]{1,0:T(8,128)(2,1)}, bf16[512,3072]{1,0:T(8,128)(2,1)}, u32[]{:S(2)}, u32[]{:S(2)}) collective-permute-start(bf16[512,3072]{1,0:T(8,128)(2,1)} %reduce-precision_convert_fusion.18), channel_id=1, source_target_pairs={{4,8},{8,4},{5,9},{9,5},{6,10},{10,6},{7,11},{11,7},{20,24},{24,20... | collective-permute-start | bytes 9437192 | tf_op jit(solution)/shard_map/ppermute | solution.py:68
  853.7 178.5 %collective-permute-start.20 = (bf16[512,3072]{1,0:T(8,128)(2,1)}, bf16[512,3072]{1,0:T(8,128)(2,1)}, u32[]{:S(2)}, u32[]{:S(2)}) collective-permute-start(bf16[512,3072]{1,0:T(8,128)(2,1)} %convolution_convert_fusion.11), channel_id=1, source_target_pairs={{0,4},{12,8},{1,5},{13,9},{2,6},{14,10},{3,7},{15,11},{16,20},{28,... | collective-permute-start | bytes 9437192 | tf_op jit(solution)/shard_map/ppermute | solution.py:64
  945.6 73.2 %collective-permute-start.19 = (bf16[512,3072]{1,0:T(8,128)(2,1)}, bf16[512,3072]{1,0:T(8,128)(2,1)}, u32[]{:S(2)}, u32[]{:S(2)}) collective-permute-start(bf16[512,3072]{1,0:T(8,128)(2,1)} %reduce-precision_convert_fusion.17), channel_id=1, source_target_pairs={{4,0},{8,12},{5,1},{9,13},{6,2},{10,14},{7,3},{11,15},{20,16},{24,... | collective-permute-start | bytes 9437192 | tf_op jit(solution)/shard_map/ppermute | solution.py:72
  986.9 113.0 %collective-permute-start.23 = (bf16[512,3072]{1,0:T(8,128)(2,1)}, bf16[512,3072]{1,0:T(8,128)(2,1)}, u32[]{:S(2)}, u32[]{:S(2)}) collective-permute-start(bf16[512,3072]{1,0:T(8,128)(2,1)} %convolution_convert_fusion.10), channel_id=1, source_target_pairs={{0,4},{12,8},{1,5},{13,9},{2,6},{14,10},{3,7},{15,11},{16,20},{28,... | collective-permute-start | bytes 9437192 | tf_op jit(solution)/shard_map/ppermute | solution.py:64
  1006.1 73.3 %collective-permute-start.21 = (bf16[512,3072]{1,0:T(8,128)(2,1)}, bf16[512,3072]{1,0:T(8,128)(2,1)}, u32[]{:S(2)}, u32[]{:S(2)}) collective-permute-start(bf16[512,3072]{1,0:T(8,128)(2,1)} %reduce-precision_convert_fusion.14), channel_id=1, source_target_pairs={{4,8},{8,4},{5,9},{9,5},{6,10},{10,6},{7,11},{11,7},{20,24},{24,20... | collective-permute-start | bytes 9437192 | tf_op jit(solution)/shard_map/ppermute | solution.py:68
  1008.6 78.1 %collective-permute-start.22 = (bf16[512,3072]{1,0:T(8,128)(2,1)}, bf16[512,3072]{1,0:T(8,128)(2,1)}, u32[]{:S(2)}, u32[]{:S(2)}) collective-permute-start(bf16[512,3072]{1,0:T(8,128)(2,1)} %reduce-precision_convert_fusion.15), channel_id=1, source_target_pairs={{4,0},{8,12},{5,1},{9,13},{6,2},{10,14},{7,3},{11,15},{20,16},{24,... | collective-permute-start | bytes 9437192 | tf_op jit(solution)/shard_map/ppermute | solution.py:72
  1018.8 173.4 %collective-permute-start.27 = (bf16[512,3072]{1,0:T(8,128)(2,1)}, bf16[512,3072]{1,0:T(8,128)(2,1)}, u32[]{:S(2)}, u32[]{:S(2)}) collective-permute-start(bf16[512,3072]{1,0:T(8,128)(2,1)} %convolution_convert_fusion.9), channel_id=1, source_target_pairs={{0,4},{12,8},{1,5},{13,9},{2,6},{14,10},{3,7},{15,11},{16,20},{28,... | collective-permute-start | bytes 9437192 | tf_op jit(solution)/shard_map/ppermute | solution.py:64
  1041.4 105.8 %collective-permute-start.24 = (bf16[512,3072]{1,0:T(8,128)(2,1)}, bf16[512,3072]{1,0:T(8,128)(2,1)}, u32[]{:S(2)}, u32[]{:S(2)}) collective-permute-start(bf16[512,3072]{1,0:T(8,128)(2,1)} %reduce-precision_convert_fusion.12), channel_id=1, source_target_pairs={{4,8},{8,4},{5,9},{9,5},{6,10},{10,6},{7,11},{11,7},{20,24},{24,20... | collective-permute-start | bytes 9437192 | tf_op jit(solution)/shard_map/ppermute | solution.py:68
  1079.4 74.6 %collective-permute-start.26 = (bf16[512,3072]{1,0:T(8,128)(2,1)}, bf16[512,3072]{1,0:T(8,128)(2,1)}, u32[]{:S(2)}, u32[]{:S(2)}) collective-permute-start(bf16[512,3072]{1,0:T(8,128)(2,1)} %reduce-precision_convert_fusion.13), channel_id=1, source_target_pairs={{4,0},{8,12},{5,1},{9,13},{6,2},{10,14},{7,3},{11,15},{20,16},{24,... | collective-permute-start | bytes 9437192 | tf_op jit(solution)/shard_map/ppermute | solution.py:72
  1086.7 179.5 %collective-permute-start.31 = (bf16[512,3072]{1,0:T(8,128)(2,1)}, bf16[512,3072]{1,0:T(8,128)(2,1)}, u32[]{:S(2)}, u32[]{:S(2)}) collective-permute-start(bf16[512,3072]{1,0:T(8,128)(2,1)} %convolution_convert_fusion.8), channel_id=1, source_target_pairs={{0,4},{12,8},{1,5},{13,9},{2,6},{14,10},{3,7},{15,11},{16,20},{28,... | collective-permute-start | bytes 9437192 | tf_op jit(solution)/shard_map/ppermute | solution.py:64
  1109.2 117.5 %collective-permute-start.28 = (bf16[512,3072]{1,0:T(8,128)(2,1)}, bf16[512,3072]{1,0:T(8,128)(2,1)}, u32[]{:S(2)}, u32[]{:S(2)}) collective-permute-start(bf16[512,3072]{1,0:T(8,128)(2,1)} %reduce-precision_convert_fusion.10), channel_id=1, source_target_pairs={{4,8},{8,4},{5,9},{9,5},{6,10},{10,6},{7,11},{11,7},{20,24},{24,20... | collective-permute-start | bytes 9437192 | tf_op jit(solution)/shard_map/ppermute | solution.py:68
  1147.2 86.6 %collective-permute-start.30 = (bf16[512,3072]{1,0:T(8,128)(2,1)}, bf16[512,3072]{1,0:T(8,128)(2,1)}, u32[]{:S(2)}, u32[]{:S(2)}) collective-permute-start(bf16[512,3072]{1,0:T(8,128)(2,1)} %reduce-precision_convert_fusion.11), channel_id=1, source_target_pairs={{4,0},{8,12},{5,1},{9,13},{6,2},{10,14},{7,3},{11,15},{20,16},{24,... | collective-permute-start | bytes 9437192 | tf_op jit(solution)/shard_map/ppermute | solution.py:72
  1153.9 146.1 %collective-permute-start.34 = (bf16[512,3072]{1,0:T(8,128)(2,1)}, bf16[512,3072]{1,0:T(8,128)(2,1)}, u32[]{:S(2)}, u32[]{:S(2)}) collective-permute-start(bf16[512,3072]{1,0:T(8,128)(2,1)} %convolution_convert_fusion.7), channel_id=1, source_target_pairs={{0,4},{12,8},{1,5},{13,9},{2,6},{14,10},{3,7},{15,11},{16,20},{28,... | collective-permute-start | bytes 9437192 | tf_op jit(solution)/shard_map/ppermute | solution.py:64
  1192.2 122.6 %collective-permute-start.25 = (bf16[512,3072]{1,0:T(8,128)(2,1)}, bf16[512,3072]{1,0:T(8,128)(2,1)}, u32[]{:S(2)}, u32[]{:S(2)}) collective-permute-start(bf16[512,3072]{1,0:T(8,128)(2,1)} %reduce-precision_convert_fusion.9), channel_id=1, source_target_pairs={{4,0},{8,12},{5,1},{9,13},{6,2},{10,14},{7,3},{11,15},{20,16},{24,... | collective-permute-start | bytes 9437192 | tf_op jit(solution)/shard_map/ppermute | solution.py:72
  1233.8 143.2 %collective-permute-start.37 = (bf16[512,3072]{1,0:T(8,128)(2,1)}, bf16[512,3072]{1,0:T(8,128)(2,1)}, u32[]{:S(2)}, u32[]{:S(2)}) collective-permute-start(bf16[512,3072]{1,0:T(8,128)(2,1)} %convolution_convert_fusion.6), channel_id=1, source_target_pairs={{0,4},{12,8},{1,5},{13,9},{2,6},{14,10},{3,7},{15,11},{16,20},{28,... | collective-permute-start | bytes 9437192 | tf_op jit(solution)/shard_map/ppermute | solution.py:64
  1266.2 176.3 %collective-permute-start.29 = (bf16[512,3072]{1,0:T(8,128)(2,1)}, bf16[512,3072]{1,0:T(8,128)(2,1)}, u32[]{:S(2)}, u32[]{:S(2)}) collective-permute-start(bf16[512,3072]{1,0:T(8,128)(2,1)} %reduce-precision_convert_fusion.7), channel_id=1, source_target_pairs={{4,0},{8,12},{5,1},{9,13},{6,2},{10,14},{7,3},{11,15},{20,16},{24,... | collective-permute-start | bytes 9437192 | tf_op jit(solution)/shard_map/ppermute | solution.py:72
  1300.0 136.4 %collective-permute-start.40 = (bf16[256,3072]{1,0:T(8,128)(2,1)}, bf16[256,3072]{1,0:T(8,128)(2,1)}, u32[]{:S(2)}, u32[]{:S(2)}) collective-permute-start(bf16[256,3072]{1,0:T(8,128)(2,1)} %get-tuple-element.298), channel_id=1, source_target_pairs={{0,4},{12,8},{1,5},{13,9},{2,6},{14,10},{3,7},{15,11},{16,20},{28,... | collective-permute-start | bytes 4718600 | tf_op jit(solution)/shard_map/ppermute | solution.py:64
  1314.8 82.4 %collective-permute-start.38 = (bf16[512,3072]{1,0:T(8,128)(2,1)}, bf16[512,3072]{1,0:T(8,128)(2,1)}, u32[]{:S(2)}, u32[]{:S(2)}) collective-permute-start(bf16[512,3072]{1,0:T(8,128)(2,1)} %reduce-precision_convert_fusion.4), channel_id=1, source_target_pairs={{4,8},{8,4},{5,9},{9,5},{6,10},{10,6},{7,11},{11,7},{20,24},{24,20... | collective-permute-start | bytes 9437192 | tf_op jit(solution)/shard_map/ppermute | solution.py:68
  1346.3 197.1 %collective-permute-start.43 = (bf16[256,3072]{1,0:T(8,128)(2,1)}, bf16[256,3072]{1,0:T(8,128)(2,1)}, u32[]{:S(2)}, u32[]{:S(2)}) collective-permute-start(bf16[256,3072]{1,0:T(8,128)(2,1)} %get-tuple-element.311), channel_id=1, source_target_pairs={{0,4},{12,8},{1,5},{13,9},{2,6},{14,10},{3,7},{15,11},{16,20},{28,... | collective-permute-start | bytes 4718600 | tf_op jit(solution)/shard_map/ppermute | solution.py:64
  1377.1 84.2 %collective-permute-start.33 = (bf16[512,3072]{1,0:T(8,128)(2,1)}, bf16[512,3072]{1,0:T(8,128)(2,1)}, u32[]{:S(2)}, u32[]{:S(2)}) collective-permute-start(bf16[512,3072]{1,0:T(8,128)(2,1)} %reduce-precision_convert_fusion.5), channel_id=1, source_target_pairs={{4,0},{8,12},{5,1},{9,13},{6,2},{10,14},{7,3},{11,15},{20,16},{24,... | collective-permute-start | bytes 9437192 | tf_op jit(solution)/shard_map/ppermute | solution.py:72
  1397.2 150.2 %collective-permute-start.46 = (bf16[128,3072]{1,0:T(8,128)(2,1)}, bf16[128,3072]{1,0:T(8,128)(2,1)}, u32[]{:S(2)}, u32[]{:S(2)}) collective-permute-start(bf16[128,3072]{1,0:T(8,128)(2,1)} %get-tuple-element.323), channel_id=1, source_target_pairs={{0,4},{12,8},{1,5},{13,9},{2,6},{14,10},{3,7},{15,11},{16,20},{28,... | collective-permute-start | bytes 2359304 | tf_op jit(solution)/shard_map/ppermute | solution.py:64
  1461.3 165.0 %collective-permute-start.49 = (bf16[128,3072]{1,0:T(8,128)(2,1)}, bf16[128,3072]{1,0:T(8,128)(2,1)}, u32[]{:S(2)}, u32[]{:S(2)}) collective-permute-start(bf16[128,3072]{1,0:T(8,128)(2,1)} %get-tuple-element.335), channel_id=1, source_target_pairs={{0,4},{12,8},{1,5},{13,9},{2,6},{14,10},{3,7},{15,11},{16,20},{28,... | collective-permute-start | bytes 2359304 | tf_op jit(solution)/shard_map/ppermute | solution.py:64
  1470.3 132.2 %collective-permute-start.36 = (bf16[512,3072]{1,0:T(8,128)(2,1)S(1)}, bf16[512,3072]{1,0:T(8,128)(2,1)S(1)}, u32[]{:S(2)}, u32[]{:S(2)}) collective-permute-start(bf16[512,3072]{1,0:T(8,128)(2,1)S(1)} %copy-done.21), channel_id=1, source_target_pairs={{4,0},{8,12},{5,1},{9,13},{6,2},{10,14},{7,3},{11,15},{20,16},{24,... | collective-permute-start | bytes 9437192 | tf_op jit(solution)/shard_map/ppermute | solution.py:72
  1474.2 155.0 %collective-permute-start.52 = (bf16[128,3072]{1,0:T(8,128)(2,1)S(1)}, bf16[128,3072]{1,0:T(8,128)(2,1)}, u32[]{:S(2)}, u32[]{:S(2)}) collective-permute-start(bf16[128,3072]{1,0:T(8,128)(2,1)S(1)} %copy-done.30), channel_id=1, source_target_pairs={{0,4},{12,8},{1,5},{13,9},{2,6},{14,10},{3,7},{15,11},{16,20},{28,... | collective-permute-start | bytes 2359304 | tf_op jit(solution)/shard_map/ppermute | solution.py:64
  1543.4 126.5 %collective-permute-start.39 = (bf16[512,3072]{1,0:T(8,128)(2,1)S(1)}, bf16[512,3072]{1,0:T(8,128)(2,1)S(1)}, u32[]{:S(2)}, u32[]{:S(2)}) collective-permute-start(bf16[512,3072]{1,0:T(8,128)(2,1)S(1)} %copy-done.19), channel_id=1, source_target_pairs={{4,0},{8,12},{5,1},{9,13},{6,2},{10,14},{7,3},{11,15},{20,16},{24,... | collective-permute-start | bytes 9437192 | tf_op jit(solution)/shard_map/ppermute | solution.py:72
  1549.0 74.0 %collective-permute-start.47 = (bf16[256,3072]{1,0:T(8,128)(2,1)S(1)}, bf16[256,3072]{1,0:T(8,128)(2,1)}, u32[]{:S(2)}, u32[]{:S(2)}) collective-permute-start(bf16[256,3072]{1,0:T(8,128)(2,1)S(1)} %reduce-precision_convert_fusion.30), channel_id=1, source_target_pairs={{4,8},{8,4},{5,9},{9,5},{6,10},{10,6},{7,11},{11,7},{20,24},{24,20... | collective-permute-start | bytes 4718600 | tf_op jit(solution)/shard_map/ppermute | solution.py:68
  1623.0 114.3 %collective-permute-start.42 = (bf16[512,3072]{1,0:T(8,128)(2,1)S(1)}, bf16[512,3072]{1,0:T(8,128)(2,1)S(1)}, u32[]{:S(2)}, u32[]{:S(2)}) collective-permute-start(bf16[512,3072]{1,0:T(8,128)(2,1)S(1)} %reduce-precision_convert_fusion), channel_id=1, source_target_pairs={{4,0},{8,12},{5,1},{9,13},{6,2},{10,14},{7,3},{11,15},{20,16},{24,... | collective-permute-start | bytes 9437192 | tf_op jit(solution)/shard_map/ppermute | solution.py:72
  1626.4 144.7 %collective-permute-start.45 = (bf16[256,3072]{1,0:T(8,128)(2,1)S(1)}, bf16[256,3072]{1,0:T(8,128)(2,1)S(1)}, u32[]{:S(2)}, u32[]{:S(2)}) collective-permute-start(bf16[256,3072]{1,0:T(8,128)(2,1)S(1)} %reduce-precision_convert_fusion.29), channel_id=1, source_target_pairs={{4,0},{8,12},{5,1},{9,13},{6,2},{10,14},{7,3},{11,15},{20,16},{24,... | collective-permute-start | bytes 4718600 | tf_op jit(solution)/shard_map/ppermute | solution.py:72
  1675.0 129.8 %collective-permute-start.48 = (bf16[256,3072]{1,0:T(8,128)(2,1)S(1)}, bf16[256,3072]{1,0:T(8,128)(2,1)S(1)}, u32[]{:S(2)}, u32[]{:S(2)}) collective-permute-start(bf16[256,3072]{1,0:T(8,128)(2,1)S(1)} %reduce-precision_convert_fusion.28), channel_id=1, source_target_pairs={{4,0},{8,12},{5,1},{9,13},{6,2},{10,14},{7,3},{11,15},{20,16},{24,... | collective-permute-start | bytes 4718600 | tf_op jit(solution)/shard_map/ppermute | solution.py:72
  1678.1 143.5 %collective-permute-start.51 = (bf16[128,3072]{1,0:T(8,128)(2,1)S(1)}, bf16[128,3072]{1,0:T(8,128)(2,1)S(1)}, u32[]{:S(2)}, u32[]{:S(2)}) collective-permute-start(bf16[128,3072]{1,0:T(8,128)(2,1)S(1)} %reduce-precision_convert_fusion.37), channel_id=1, source_target_pairs={{4,0},{8,12},{5,1},{9,13},{6,2},{10,14},{7,3},{11,15},{20,16},{24,... | collective-permute-start | bytes 2359304 | tf_op jit(solution)/shard_map/ppermute | solution.py:72
  1680.8 157.7 %collective-permute-start.54 = (bf16[128,3072]{1,0:T(8,128)(2,1)S(1)}, bf16[128,3072]{1,0:T(8,128)(2,1)S(1)}, u32[]{:S(2)}, u32[]{:S(2)}) collective-permute-start(bf16[128,3072]{1,0:T(8,128)(2,1)S(1)} %reduce-precision_convert_fusion.35), channel_id=1, source_target_pairs={{4,0},{8,12},{5,1},{9,13},{6,2},{10,14},{7,3},{11,15},{20,16},{24,... | collective-permute-start | bytes 2359304 | tf_op jit(solution)/shard_map/ppermute | solution.py:72
  1741.6 111.9 %collective-permute-start.56 = (bf16[128,3072]{1,0:T(8,128)(2,1)S(1)}, bf16[128,3072]{1,0:T(8,128)(2,1)S(1)}, u32[]{:S(2)}, u32[]{:S(2)}) collective-permute-start(bf16[128,3072]{1,0:T(8,128)(2,1)S(1)} %reduce-precision_convert_fusion.34), channel_id=1, source_target_pairs={{4,0},{8,12},{5,1},{9,13},{6,2},{10,14},{7,3},{11,15},{20,16},{24,... | collective-permute-start | bytes 2359304 | tf_op jit(solution)/shard_map/ppermute | solution.py:72
  1771.1 90.9 %collective-permute-start.59 = (bf16[128,3072]{1,0:T(8,128)(2,1)S(1)}, bf16[128,3072]{1,0:T(8,128)(2,1)S(1)}, u32[]{:S(2)}, u32[]{:S(2)}) collective-permute-start(bf16[128,3072]{1,0:T(8,128)(2,1)S(1)} %reduce-precision_convert_fusion.32), channel_id=1, source_target_pairs={{4,0},{8,12},{5,1},{9,13},{6,2},{10,14},{7,3},{11,15},{20,16},{24,... | collective-permute-start | bytes 2359304 | tf_op jit(solution)/shard_map/ppermute | solution.py:72
  (86 other events, 2256.9 us)
Sparse Core Ops, SparseCore 0:
  9.6 58.0 all-gather.5
  69.2 37.4 all-gather.7
  108.2 82.0 all-gather.9
  192.3 82.0 all-gather.11
  275.8 82.0 all-gather.13
